TPU v7x, 32 devices: a whole 2x2x4 slice. The times are simulated.
32 devices in a mesh: cuts: 4 (over z), tile: 8 (over y, x, core).
Axes of the slice: x: 2, y: 2, z: 4, core: 2. Of those that a mesh axis runs over, the one named last changes fastest.
Arguments:
- probe_wave: float32 [2, 256, 256], replicated, may hold values from -6 to 6
- transmission: float32 [4, 2, 4096, 2048], P('cuts', None, None, 'tile'), may hold values from -1 to 1, as said below
- kernel_phase: float32 [256, 256], replicated, may hold values from -3.140625 to 3.140625
- measured: bfloat16 [8, 6, 256, 256], P('tile'), may hold values from 0 to 4
- counts: int32 [8], P('tile'), may hold values from 1 to 6, as said below
- positions: int32 [8, 6, 2], P('tile'), may hold values from 0 to 3840, as said below
- widths: int32 [8, 2], P('tile'), may hold values from 32 to 128
Outputs:
- adjoint_wave: float32 [4, 8, 6, 2, 256, 256], P('cuts', 'tile')
- object_grad: float32 [4, 2, 4096, 2048], P('cuts', None, None, 'tile')
Inputs may be any that keep to these rules, and one draw needn't show every extreme that they name: Every entry has magnitude at most 1; each pair is a complex transmission. Tile t uses its first counts[t] slots; some tile uses all 6 slots. `positions`: rows lie in 0 to 3840 and columns in 0 to 256; column 0 of a tile's extended patch is 128 columns left of its first own column.
All inputs are finite; a program needn't handle non-finite values.
Results may differ from a plain program's by a relative error of at most 0.0003.
Values sent between devices are 32-bit elements; how exact they have to be, the bound alone decides.
A program may use at most 256 MiB of HBM per device.

v0:
```python
import math

import jax
import jax.numpy as jnp
from jax import lax
from jax.sharding import PartitionSpec as P

RIM = 128


def extended(value, sides, width):
    for axis, dim in sides:
        count, length = (lax.axis_size(axis), value.shape[dim])
        up = [(i, (i + 1) % count) for i in range(count - 1)]
        down = [(j, i) for i, j in up]
        last = lax.slice_in_dim(value, length - width, length, axis=dim)
        initial = lax.slice_in_dim(value, 0, width, axis=dim)
        before = lax.ppermute(last, axis, up)
        after = lax.ppermute(initial, axis, down)
        value = jnp.concatenate([before, value, after], axis=dim)
    return value


def from_behind(value, axis, by):
    count = lax.axis_size(axis)
    pairs = [(i, i + by) for i in range(count) if 0 <= i + by < count]
    return lax.ppermute(value, axis, pairs)


def make_tables(extent):
    indices = jnp.arange(extent, dtype=jnp.int32)
    product = indices[:, None] * indices[None, :] % extent
    angles = product.astype(jnp.float32) * (2.0 * math.pi / extent)
    cosine = jnp.cos(angles) / math.sqrt(extent)
    sine_part = jnp.sin(angles) / math.sqrt(extent)
    forward = jnp.concatenate(
        [jnp.concatenate([cosine, sine_part], 1), jnp.concatenate([-sine_part, cosine], 1)], 0
    )
    inverse = jnp.concatenate(
        [jnp.concatenate([cosine, -sine_part], 1), jnp.concatenate([sine_part, cosine], 1)], 0
    )
    return (forward, inverse)


def transform(fields, matrix):
    number = fields.shape[0]
    extent = fields.shape[-1]
    stacked = fields.reshape(number, 2 * extent, extent)
    halfway = jnp.einsum("ab,pbc->pac", matrix, stacked, precision=lax.Precision.HIGHEST)
    halfway = halfway.reshape(number, 2, extent, extent)
    quadrant = matrix.reshape(2, extent, 2, extent)
    return jnp.einsum("psik,rjsk->prij", halfway, quadrant, precision=lax.Precision.HIGHEST)


def complex_mul(first_op, second_op):
    first_re, first_im = (first_op[..., 0, :, :], first_op[..., 1, :, :])
    second_re, second_im = (second_op[..., 0, :, :], second_op[..., 1, :, :])
    return jnp.stack(
        [first_re * second_re - first_im * second_im, first_re * second_im + first_im * second_re],
        axis=-3,
    )


def conj_mul(first_op, second_op):
    first_re, first_im = (first_op[..., 0, :, :], first_op[..., 1, :, :])
    second_re, second_im = (second_op[..., 0, :, :], second_op[..., 1, :, :])
    return jnp.stack(
        [first_re * second_re + first_im * second_im, first_re * second_im - first_im * second_re],
        axis=-3,
    )


def propagate(fields, kernel, tables):
    spectrum = transform(fields, tables[0])
    return transform(complex_mul(kernel, spectrum), tables[1])


def keep_columns(tile_at, width_pair, tiles_total, owned_cols, margin):
    columns = jnp.arange(owned_cols + 2 * margin, dtype=jnp.int32)
    globally = tile_at * owned_cols - margin + columns
    inside = (globally >= 0) & (globally < tiles_total * owned_cols)
    middle = (columns >= margin) & (columns < margin + owned_cols)
    left_ok = (columns < margin) & (margin - columns <= width_pair[0])
    right_ok = (columns >= margin + owned_cols) & (
        columns - margin - owned_cols + 1 <= width_pair[1]
    )
    return inside & (middle | left_ok | right_ok)


def cut_windows(grad_plane, places, extent):
    anchor = jnp.zeros((), jnp.int32)

    def single(corner):
        return lax.dynamic_slice(grad_plane, (anchor, corner[0], corner[1]), (2, extent, extent))

    return jax.vmap(single)(places)


def add_windows(grad_plane, places, contrib, extent):
    anchor = jnp.zeros((), jnp.int32)
    corner_at = (anchor, places[0, 0], places[0, 1])
    current = lax.dynamic_slice(grad_plane, corner_at, (2, extent, extent))
    grad_plane = lax.dynamic_update_slice(grad_plane, current + contrib[0], corner_at)
    return grad_plane


def on_device(probe_wave, transmission, kernel_phase, measured, counts, positions, widths):
    slices_here = transmission.shape[0]
    owned_cols = transmission.shape[3]
    extent = probe_wave.shape[-1]
    margin = RIM
    sections = lax.axis_size("cuts")
    section_at = lax.axis_index("cuts")
    tile_at = lax.axis_index("tile")
    tiles_total = lax.axis_size("tile")
    capacity = positions.shape[1]
    last_section = sections - 1
    tables = make_tables(extent)
    kernel = jnp.stack([jnp.cos(kernel_phase), jnp.sin(kernel_phase)], 0)
    kernel_conj = jnp.stack([jnp.cos(kernel_phase), -jnp.sin(kernel_phase)], 0)
    vacuum = jnp.array([1.0, 0.0], dtype=jnp.float32)[:, None, None]
    object_patch = extended(transmission, (("tile", 3),), margin)
    keep_mask = keep_columns(tile_at, widths[0], tiles_total, owned_cols, margin)
    object_patch = jnp.where(keep_mask, object_patch, vacuum)
    places = positions[0]
    live_slots = (jnp.arange(capacity, dtype=jnp.int32) < counts[0]).astype(jnp.float32)
    entering = probe_wave[None] * live_slots[:, None, None, None]
    members = capacity // capacity
    rounds = capacity + sections - 1
    wave_shape = (members, 2, extent, extent)

    def run_forward(fields, spot_rows):
        windows = cut_windows(object_patch[0], spot_rows, extent)
        inputs = [fields]
        fields = propagate(complex_mul(windows, fields), kernel, tables)
        return (jnp.stack(inputs, 0), fields)

    def skip_forward(fields, spot_rows):
        return (
            jnp.zeros((slices_here,) + wave_shape, jnp.float32),
            jnp.zeros(wave_shape, jnp.float32),
        )

    saved_waves = jnp.zeros((capacity + 1, slices_here) + wave_shape, jnp.float32)
    exit_waves = jnp.zeros((capacity + 1,) + wave_shape, jnp.float32)
    arriving = jnp.zeros(wave_shape, jnp.float32)
    for round_at in range(rounds):
        batch_at = round_at - section_at
        is_valid = (batch_at >= 0) & (batch_at < capacity)
        slot_at = jnp.where(is_valid, batch_at, capacity)
        first_row = jnp.clip(batch_at, 0, capacity - 1) * members
        fields = jnp.where(
            section_at == 0, lax.dynamic_slice_in_dim(entering, first_row, members, 0), arriving
        )
        spot_rows = lax.dynamic_slice_in_dim(places, first_row, members, 0)
        inputs, leaving = lax.cond(is_valid, run_forward, skip_forward, fields, spot_rows)
        saved_waves = lax.dynamic_update_slice_in_dim(saved_waves, inputs[None], slot_at, 0)
        exit_waves = lax.dynamic_update_slice_in_dim(exit_waves, leaving[None], slot_at, 0)
        if round_at + 1 < rounds:
            arriving = from_behind(leaving, "cuts", 1)

    def run_adjoint(grad_ext, fields, inputs, spot_rows):
        for slice_at in reversed(range(slices_here)):
            turned = propagate(fields, kernel_conj, tables)
            contrib = conj_mul(inputs[slice_at], turned)
            grad_plane = add_windows(grad_ext[slice_at], spot_rows, contrib, extent)
            grad_ext = grad_ext.at[slice_at].set(grad_plane)
            windows = cut_windows(object_patch[slice_at], spot_rows, extent)
            fields = conj_mul(windows, turned)
        return (grad_ext, fields)

    def skip_adjoint(grad_ext, fields, inputs, spot_rows):
        return (grad_ext, jnp.zeros(wave_shape, jnp.float32))

    def far_adjoint(fields, observed):
        far_field = transform(fields, tables[0])
        intensity = far_field[:, 0] * far_field[:, 0] + far_field[:, 1] * far_field[:, 1]
        residual = intensity - observed.astype(jnp.float32)
        return transform(far_field * residual[:, None], tables[1])

    def skip_far(fields, observed):
        return jnp.zeros(wave_shape, jnp.float32)

    grad_ext = jnp.zeros(object_patch.shape, jnp.float32)
    adjoints = jnp.zeros((capacity + 1,) + wave_shape, jnp.float32)
    arriving = jnp.zeros(wave_shape, jnp.float32)
    for round_at in range(rounds):
        batch_at = round_at - (last_section - section_at)
        is_valid = (batch_at >= 0) & (batch_at < capacity)
        slot_at = jnp.where(is_valid, batch_at, capacity)
        clipped = jnp.clip(batch_at, 0, capacity - 1)
        first_row = clipped * members
        spot_rows = lax.dynamic_slice_in_dim(places, first_row, members, 0)
        observed = lax.dynamic_slice_in_dim(measured[0], first_row, members, 0)
        exit_now = lax.dynamic_index_in_dim(exit_waves, clipped, 0, keepdims=False)
        starting = lax.cond(
            is_valid & (section_at == last_section), far_adjoint, skip_far, exit_now, observed
        )
        fields = jnp.where(section_at == last_section, starting, arriving)
        inputs = lax.dynamic_index_in_dim(saved_waves, clipped, 0, keepdims=False)
        grad_ext, backward = lax.cond(
            is_valid, run_adjoint, skip_adjoint, grad_ext, fields, inputs, spot_rows
        )
        adjoints = lax.dynamic_update_slice_in_dim(adjoints, backward[None], slot_at, 0)
        if round_at + 1 < rounds:
            arriving = from_behind(backward, "cuts", -1)
    adjoint_wave = adjoints[:capacity].reshape((capacity, 2, extent, extent))[None, None]
    grad_ext = jnp.where(keep_mask, grad_ext, 0.0)
    rim_pair = jnp.concatenate([grad_ext[..., :margin], grad_ext[..., margin + owned_cols :]], 3)
    widened = extended(rim_pair, (("tile", 3),), margin)
    center = grad_ext[..., margin : margin + owned_cols]
    center = center.at[..., :margin].add(widened[..., :margin])
    center = center.at[..., owned_cols - margin :].add(widened[..., 3 * margin :])
    return (adjoint_wave, center)


def solution(mesh):
    return jax.shard_map(
        on_device,
        mesh=mesh,
        in_specs=(
            P(),
            P("cuts", None, None, "tile"),
            P(),
            P("tile", None, None, None),
            P("tile"),
            P("tile", None, None),
            P("tile", None),
        ),
        out_specs=(P("cuts", "tile", None, None, None, None), P("cuts", None, None, "tile")),
        check_vma=False,
    )
```

profile of v0, /device:TPU:3, one launch (start us, length us, event | category | flops | bytes accessed | tf_op | source)
XLA Modules:
  0.0 1098.2 jit_solution(9915959346858189614)
XLA Ops:
  0.6 7.4 fusion.146
  22.5 79.7 %collective-permute-done.1 = f32[1,2,4096,128]{3,2,1,0:T(8,128)} collective-permute-done((f32[1,2,4096,128]{3,2,1,0:T(8,128)}, f32[1,2,4096,128]{3,2,1,0:T(8,128)}, u32[]{:S(2)}, u32[]{:S(2)}) %collective-permute-start.1) | collective-permute-done | bytes 4194336 | tf_op jit(solution)/shard_map/ppermute | solution.py:19
  102.2 12.0 %maximum_select_fusion = f32[1,2,4096,512]{3,2,1,0:T(8,128)} fusion(f32[1,2,4096,128]{3,2,1,0:T(8,128)} %collective-permute-done.1, f32[1,2,4096,256]{3,2,1,0:T(8,128)} %param.85, f32[1,2,4096,128]{3,2,1,0:T(8,128)} %collective-permute-done, f32[2]{0:T(128)S(1)} %copy-done.20, pred[512]{0:T(512)(128)(4,1)S(1)} %fusion.121), kind=kLoop, calls=%fused_computation.450 | loop fusion | flops 12582912 | bytes 33554952 | tf_op jit(solution)/shard_map/jit(_where)/select_n | solution.py:124
  115.1 28.2 %conditional.27 = (f32[1,2,256,256]{3,2,1,0:T(8,128)}, f32[1,1,1,2,256,256]{5,4,3,2,1,0:T(8,128)S(1)}, f32[1,1,2,256,256]{4,3,2,1,0:T(8,128)}) conditional(s32[]{:T(128)} %convert_element_type.187, () %tuple.413, (f32[1,2,4096,512]{3,2,1,0:T(8,128)}, s32[]{:T(128)}, s32[1,6,2]{1,2,0:T(2,128)S(1)}, f32[6,2,256,256]{3,2,1,0:T(8,128)}, ...), branch_computations={%region_0.1_spmd, %region_1.2_spmd} | conditional | flops 3222405120 | bytes 26870092 | solution.py:156
  145.3 7.6 collective-permute-done.2
  152.9 28.8 %conditional.28 = (f32[1,2,256,256]{3,2,1,0:T(8,128)}, f32[1,1,1,2,256,256]{5,4,3,2,1,0:T(8,128)}, f32[1,1,2,256,256]{4,3,2,1,0:T(8,128)}) conditional(s32[]{:T(128)} %convert_element_type.190, () %tuple.415, (f32[1,2,4096,512]{3,2,1,0:T(8,128)}, s32[]{:T(128)}, s32[1,6,2]{1,2,0:T(2,128)S(1)}, f32[6,2,256,256]{3,2,1,0:T(8,128)}, ...), branch_computations={%region_2.3_spmd, %region_3.4_spmd} | conditional | flops 3222405120 | bytes 22675732 | solution.py:156
  186.4 8.7 collective-permute-done.3
  195.1 28.4 %conditional.29 = (f32[1,2,256,256]{3,2,1,0:T(8,128)}, f32[1,1,1,2,256,256]{5,4,3,2,1,0:T(8,128)}, f32[1,1,2,256,256]{4,3,2,1,0:T(8,128)}) conditional(s32[]{:T(128)} %convert_element_type.191, () %tuple.417, (f32[1,2,4096,512]{3,2,1,0:T(8,128)}, s32[]{:T(128)}, s32[1,6,2]{1,2,0:T(2,128)S(1)}, f32[6,2,256,256]{3,2,1,0:T(8,128)}, ...), branch_computations={%region_4.5_spmd, %region_5.6_spmd} | conditional | flops 3222405120 | bytes 22675732 | solution.py:156
  228.3 9.7 collective-permute-done.4
  237.9 28.3 %conditional.30 = (f32[1,2,256,256]{3,2,1,0:T(8,128)}, f32[1,1,1,2,256,256]{5,4,3,2,1,0:T(8,128)}, f32[1,1,2,256,256]{4,3,2,1,0:T(8,128)}) conditional(s32[]{:T(128)} %convert_element_type.192, () %tuple.419, (f32[1,2,4096,512]{3,2,1,0:T(8,128)}, s32[]{:T(128)}, s32[1,6,2]{1,2,0:T(2,128)S(1)}, f32[6,2,256,256]{3,2,1,0:T(8,128)}, ...), branch_computations={%region_6.7_spmd, %region_7.8_spmd} | conditional | flops 3222405120 | bytes 22675732 | solution.py:156
  271.2 10.7 collective-permute-done.5
  281.8 28.5 %conditional.31 = (f32[1,2,256,256]{3,2,1,0:T(8,128)}, f32[1,1,1,2,256,256]{5,4,3,2,1,0:T(8,128)}, f32[1,1,2,256,256]{4,3,2,1,0:T(8,128)}) conditional(s32[]{:T(128)} %convert_element_type.193, () %tuple.421, (f32[1,2,4096,512]{3,2,1,0:T(8,128)}, s32[]{:T(128)}, s32[1,6,2]{1,2,0:T(2,128)S(1)}, f32[6,2,256,256]{3,2,1,0:T(8,128)}, ...), branch_computations={%region_8.9_spmd, %region_9.10_spmd} | conditional | flops 3222405120 | bytes 22675732 | solution.py:156
  325.4 28.4 %conditional.32 = (f32[1,2,256,256]{3,2,1,0:T(8,128)}, f32[1,1,1,2,256,256]{5,4,3,2,1,0:T(8,128)S(1)}, f32[1,1,2,256,256]{4,3,2,1,0:T(8,128)}) conditional(s32[]{:T(128)} %convert_element_type.194, () %tuple.423, (f32[1,2,4096,512]{3,2,1,0:T(8,128)}, s32[]{:T(128)}, s32[1,6,2]{1,2,0:T(2,128)S(1)}, f32[6,2,256,256]{3,2,1,0:T(8,128)}, ...), branch_computations={%region_10.11_spmd, %region_11.12_spmd} | conditional | flops 3222405120 | bytes 28967272 | solution.py:156
  370.8 30.5 %collective-permute-start.8 = (f32[1,2,256,256]{3,2,1,0:T(8,128)}, f32[1,2,256,256]{3,2,1,0:T(8,128)}, u32[]{:S(2)}, u32[]{:S(2)}) collective-permute-start(f32[1,2,256,256]{3,2,1,0:T(8,128)} %get-tuple-element.2297), channel_id=1, source_target_pairs={{0,8},{8,16},{16,24},{1,9},{9,17},{17,25},{2,10},{10,18},{18,26},{... | collective-permute-start | bytes 1572872 | tf_op jit(solution)/shard_map/ppermute | solution.py:27
  432.6 9.8 conditional.37
  432.6 7.9 broadcast_in_dim.421
  448.2 32.1 %collective-permute-done.10 = f32[1,2,256,256]{3,2,1,0:T(8,128)} collective-permute-done((f32[1,2,256,256]{3,2,1,0:T(8,128)}, f32[1,2,256,256]{3,2,1,0:T(8,128)}, u32[]{:S(2)}, u32[]{:S(2)}) %collective-permute-start.10) | collective-permute-done | bytes 524320 | tf_op jit(solution)/shard_map/ppermute | solution.py:27
  498.0 11.0 %conditional.42 = (f32[1,2,256,256]{3,2,1,0:T(8,128)S(1)}) conditional(s32[]{:T(128)} %convert_element_type.204, () %tuple.440, (f32[7,1,2,256,256]{4,3,2,0,1:T(8,128)}, s32[]{:T(128)}, f32[512,512]{1,0:T(8,128)S(1)}, bf16[1,6,256,256]{3,2,1,0:T(8,128)(2,1)}, f32[512,512]{1,0:T(8,128)S(1)}) %tuple.441), branch_computations={%region_30.31_spmd, %region_31.32_spmd} | conditional | flops 3221684224 | bytes 17956880 | solution.py:196
  509.1 150.9 %collective-permute-done.12 = f32[1,2,256,256]{3,2,1,0:T(8,128)} collective-permute-done((f32[1,2,256,256]{3,2,1,0:T(8,128)}, f32[1,2,256,256]{3,2,1,0:T(8,128)}, u32[]{:S(2)}, u32[]{:S(2)}) %collective-permute-start.12) | collective-permute-done | bytes 524320 | tf_op jit(solution)/shard_map/ppermute | solution.py:27
  660.0 39.3 %conditional.43 = (f32[1,2,4096,512]{3,2,1,0:T(8,128)}, f32[1,2,256,256]{3,2,1,0:T(8,128)}, f32[1,1,2,256,256]{4,3,2,1,0:T(8,128)}) conditional(s32[]{:T(128)} %convert_element_type.203, f32[1,2,4096,512]{3,2,1,0:T(8,128)} %get-tuple-element.2317, (s32[1,6,2]{1,2,0:T(2,128)S(1)}, s32[]{:T(128)}, f32[1,2,4096,512]{3,2,1,0:T(8,128)}, ...), branch_computations={%region_32.33_spmd, %region_33.34_spmd} | conditional | flops 3223060480 | bytes 27394376 | solution.py:201
  707.6 13.1 %collective-permute-done.13 = f32[1,2,256,256]{3,2,1,0:T(8,128)} collective-permute-done((f32[1,2,256,256]{3,2,1,0:T(8,128)}, f32[1,2,256,256]{3,2,1,0:T(8,128)}, u32[]{:S(2)}, u32[]{:S(2)}) %collective-permute-start.13) | collective-permute-done | bytes 524320 | tf_op jit(solution)/shard_map/ppermute | solution.py:27
  720.7 39.6 %conditional.45 = (f32[1,2,4096,512]{3,2,1,0:T(8,128)}, f32[1,2,256,256]{3,2,1,0:T(8,128)}, f32[1,1,2,256,256]{4,3,2,1,0:T(8,128)}) conditional(s32[]{:T(128)} %convert_element_type.205, f32[1,2,4096,512]{3,2,1,0:T(8,128)} %get-tuple-element.2320, (s32[1,6,2]{1,2,0:T(2,128)S(1)}, s32[]{:T(128)}, f32[1,2,4096,512]{3,2,1,0:T(8,128)}, ...), branch_computations={%region_36.37_spmd, %region_37.38_spmd} | conditional | flops 3223060480 | bytes 27394376 | solution.py:201
  768.5 10.7 collective-permute-done.14
  779.2 39.5 %conditional.47 = (f32[1,2,4096,512]{3,2,1,0:T(8,128)}, f32[1,2,256,256]{3,2,1,0:T(8,128)}, f32[1,1,2,256,256]{4,3,2,1,0:T(8,128)}) conditional(s32[]{:T(128)} %convert_element_type.207, f32[1,2,4096,512]{3,2,1,0:T(8,128)} %get-tuple-element.2323, (s32[1,6,2]{1,2,0:T(2,128)S(1)}, s32[]{:T(128)}, f32[1,2,4096,512]{3,2,1,0:T(8,128)}, ...), branch_computations={%region_40.41_spmd, %region_41.42_spmd} | conditional | flops 3223060480 | bytes 27394376 | solution.py:201
  820.6 17.8 %collective-permute-done.15 = f32[1,2,256,256]{3,2,1,0:T(8,128)} collective-permute-done((f32[1,2,256,256]{3,2,1,0:T(8,128)}, f32[1,2,256,256]{3,2,1,0:T(8,128)}, u32[]{:S(2)}, u32[]{:S(2)}) %collective-permute-start.15) | collective-permute-done | bytes 524320 | tf_op jit(solution)/shard_map/ppermute | solution.py:27
  838.3 39.7 %conditional.49 = (f32[1,2,4096,512]{3,2,1,0:T(8,128)}, f32[1,2,256,256]{3,2,1,0:T(8,128)}, f32[1,1,2,256,256]{4,3,2,1,0:T(8,128)}) conditional(s32[]{:T(128)} %convert_element_type.209, f32[1,2,4096,512]{3,2,1,0:T(8,128)} %get-tuple-element.2326, (s32[1,6,2]{1,2,0:T(2,128)S(1)}, s32[]{:T(128)}, f32[1,2,4096,512]{3,2,1,0:T(8,128)}, ...), branch_computations={%region_44.45_spmd, %region_45.46_spmd} | conditional | flops 3223060480 | bytes 27394376 | solution.py:201
  879.6 16.9 %collective-permute-done.16 = f32[1,2,256,256]{3,2,1,0:T(8,128)} collective-permute-done((f32[1,2,256,256]{3,2,1,0:T(8,128)}, f32[1,2,256,256]{3,2,1,0:T(8,128)}, u32[]{:S(2)}, u32[]{:S(2)}) %collective-permute-start.16) | collective-permute-done | bytes 524320 | tf_op jit(solution)/shard_map/ppermute | solution.py:27
  896.6 39.5 %conditional.51 = (f32[1,2,4096,512]{3,2,1,0:T(8,128)}, f32[1,2,256,256]{3,2,1,0:T(8,128)}, f32[1,1,2,256,256]{4,3,2,1,0:T(8,128)}) conditional(s32[]{:T(128)} %convert_element_type.211, f32[1,2,4096,512]{3,2,1,0:T(8,128)} %get-tuple-element.2329, (s32[1,6,2]{1,2,0:T(2,128)S(1)}, s32[]{:T(128)}, f32[1,2,4096,512]{3,2,1,0:T(8,128)}, ...), branch_computations={%region_48.49_spmd, %region_49.50_spmd} | conditional | flops 3223060480 | bytes 27394376 | solution.py:201
  937.9 17.6 %collective-permute-done.17 = f32[1,2,256,256]{3,2,1,0:T(8,128)} collective-permute-done((f32[1,2,256,256]{3,2,1,0:T(8,128)}, f32[1,2,256,256]{3,2,1,0:T(8,128)}, u32[]{:S(2)}, u32[]{:S(2)}) %collective-permute-start.17) | collective-permute-done | bytes 524320 | tf_op jit(solution)/shard_map/ppermute | solution.py:27
  955.5 31.3 %conditional.53 = (f32[1,2,4096,512]{3,2,1,0:T(8,128)}, f32[1,1,2,256,256]{4,3,2,1,0:T(8,128)S(1)}) conditional(s32[]{:T(128)} %convert_element_type.213, f32[1,2,4096,512]{3,2,1,0:T(8,128)} %get-tuple-element.2332, (s32[1,6,2]{1,2,0:T(2,128)S(1)}, s32[]{:T(128)}, f32[1,2,4096,512]{3,2,1,0:T(8,128)}, f32[7,1,1,2,256,256]{5,4,3,2,1,0:T(8,128)}, ...), branch_computations={%region_52.53_spmd, %region_53.54_spmd} | conditional | flops 3223060480 | bytes 26345792 | solution.py:201
  986.8 7.1 broadcast_select_fusion
  1023.4 64.2 %collective-permute-done.18 = f32[1,2,4096,128]{3,2,1,0:T(8,128)} collective-permute-done((f32[1,2,4096,128]{3,2,1,0:T(8,128)}, f32[1,2,4096,128]{3,2,1,0:T(8,128)}, u32[]{:S(2)}, u32[]{:S(2)}) %collective-permute-start.18) | collective-permute-done | bytes 4194336 | tf_op jit(solution)/shard_map/ppermute | solution.py:18
  (360 shorter events, 521.0 us)
Async XLA Ops:
  0.6 14.7 %copy-start.19 = (s32[1,2]{1,0:T(1,128)S(1)}, s32[1,2]{1,0:T(1,128)}, u32[]{:S(2)}) copy-start(s32[1,2]{1,0:T(1,128)} %param.90) | copy-start | bytes 28
  8.0 11.4 %copy-start.16 = (f32[256,256]{1,0:T(8,128)S(1)}, f32[256,256]{1,0:T(8,128)}, u32[]{:S(2)}) copy-start(f32[256,256]{1,0:T(8,128)} %param.86) | copy-start | bytes 786436
  8.0 12.4 %copy-start.14 = (f32[2,256,256]{2,1,0:T(8,128)S(1)}, f32[2,256,256]{2,1,0:T(8,128)}, u32[]{:S(2)}) copy-start(f32[2,256,256]{2,1,0:T(8,128)} %param.84) | copy-start | bytes 1572868
  8.0 94.1 %collective-permute-start.1 = (f32[1,2,4096,128]{3,2,1,0:T(8,128)}, f32[1,2,4096,128]{3,2,1,0:T(8,128)}, u32[]{:S(2)}, u32[]{:S(2)}) collective-permute-start(f32[1,2,4096,128]{3,2,1,0:T(8,128)} %get-tuple-element.2939), channel_id=1, source_target_pairs={{1,0},{2,1},{3,2},{4,3},{5,4},{6,5},{7,6},{9,8},{10,9},{11,10},{12... | collective-permute-start | bytes 12582920 | tf_op jit(solution)/shard_map/ppermute | solution.py:19
  10.8 91.4 %collective-permute-start = (f32[1,2,4096,128]{3,2,1,0:T(8,128)}, f32[1,2,4096,128]{3,2,1,0:T(8,128)}, u32[]{:S(2)}, u32[]{:S(2)}) collective-permute-start(f32[1,2,4096,128]{3,2,1,0:T(8,128)} %get-tuple-element.2938), channel_id=1, source_target_pairs={{0,1},{1,2},{2,3},{3,4},{4,5},{5,6},{6,7},{8,9},{9,10},{10,11},{11... | collective-permute-start | bytes 12582920 | tf_op jit(solution)/shard_map/ppermute | solution.py:18
  17.2 85.0 %copy-start.17 = (pred[512]{0:T(512)(128)(4,1)}, pred[512]{0:T(512)(128)(4,1)S(1)}, u32[]{:S(2)}) copy-start(pred[512]{0:T(512)(128)(4,1)S(1)} %fusion.121) | copy-start | bytes 1540
  19.2 82.9 %copy-start.20 = (f32[2]{0:T(128)S(1)}, f32[2]{0:T(128)}, u32[]{:S(2)}) copy-start(f32[2]{0:T(128)} %constant.1122.clone) | copy-start | bytes 28
  22.5 92.6 %copy-start.15 = (s32[1,6,2]{1,2,0:T(2,128)S(1)}, s32[1,6,2]{1,2,0:T(2,128)}, u32[]{:S(2)}) copy-start(s32[1,6,2]{1,2,0:T(2,128)} %param.89) | copy-start | bytes 148
  116.6 12.5 %copy-start.4 = (f32[1,2,256,256]{3,2,1,0:T(8,128)}, f32[1,2,256,256]{3,2,1,0:T(8,128)S(1)}, u32[]{:S(2)}) copy-start(f32[1,2,256,256]{3,2,1,0:T(8,128)S(1)} %dynamic-slice_select_fusion) | copy-start | bytes 1572868 | tf_op jit(solution)/shard_map/cond
  134.3 8.9 copy-start.5
  143.2 9.7 collective-permute-start.2
  181.7 13.3 %collective-permute-start.3 = (f32[1,2,256,256]{3,2,1,0:T(8,128)}, f32[1,2,256,256]{3,2,1,0:T(8,128)}, u32[]{:S(2)}, u32[]{:S(2)}) collective-permute-start(f32[1,2,256,256]{3,2,1,0:T(8,128)} %get-tuple-element.2287), channel_id=1, source_target_pairs={{0,8},{8,16},{16,24},{1,9},{9,17},{17,25},{2,10},{10,18},{18,26},{... | collective-permute-start | bytes 1572872 | tf_op jit(solution)/shard_map/ppermute | solution.py:27
  223.5 14.5 %collective-permute-start.4 = (f32[1,2,256,256]{3,2,1,0:T(8,128)}, f32[1,2,256,256]{3,2,1,0:T(8,128)}, u32[]{:S(2)}, u32[]{:S(2)}) collective-permute-start(f32[1,2,256,256]{3,2,1,0:T(8,128)} %get-tuple-element.2289), channel_id=1, source_target_pairs={{0,8},{8,16},{16,24},{1,9},{9,17},{17,25},{2,10},{10,18},{18,26},{... | collective-permute-start | bytes 1572872 | tf_op jit(solution)/shard_map/ppermute | solution.py:27
  266.2 15.6 %collective-permute-start.5 = (f32[1,2,256,256]{3,2,1,0:T(8,128)}, f32[1,2,256,256]{3,2,1,0:T(8,128)}, u32[]{:S(2)}, u32[]{:S(2)}) collective-permute-start(f32[1,2,256,256]{3,2,1,0:T(8,128)} %get-tuple-element.2291), channel_id=1, source_target_pairs={{0,8},{8,16},{16,24},{1,9},{9,17},{17,25},{2,10},{10,18},{18,26},{... | collective-permute-start | bytes 1572872 | tf_op jit(solution)/shard_map/ppermute | solution.py:27
  310.3 15.1 %collective-permute-start.6 = (f32[1,2,256,256]{3,2,1,0:T(8,128)}, f32[1,2,256,256]{3,2,1,0:T(8,128)S(1)}, u32[]{:S(2)}, u32[]{:S(2)}) collective-permute-start(f32[1,2,256,256]{3,2,1,0:T(8,128)} %get-tuple-element.2293), channel_id=1, source_target_pairs={{0,8},{8,16},{16,24},{1,9},{9,17},{17,25},{2,10},{10,18},{18,26},{... | collective-permute-start | bytes 1572872 | tf_op jit(solution)/shard_map/ppermute | solution.py:27
  327.5 12.1 %copy-start.6 = (f32[1,2,256,256]{3,2,1,0:T(8,128)}, f32[1,2,256,256]{3,2,1,0:T(8,128)S(1)}, u32[]{:S(2)}) copy-start(f32[1,2,256,256]{3,2,1,0:T(8,128)S(1)} %dynamic-slice_select_fusion.5) | copy-start | bytes 1572868 | tf_op jit(solution)/shard_map/cond
  344.8 9.0 copy-start.7
  353.8 14.3 %collective-permute-start.7 = (f32[1,2,256,256]{3,2,1,0:T(8,128)}, f32[1,2,256,256]{3,2,1,0:T(8,128)}, u32[]{:S(2)}, u32[]{:S(2)}) collective-permute-start(f32[1,2,256,256]{3,2,1,0:T(8,128)} %get-tuple-element.2295), channel_id=1, source_target_pairs={{0,8},{8,16},{16,24},{1,9},{9,17},{17,25},{2,10},{10,18},{18,26},{... | collective-permute-start | bytes 1572872 | tf_op jit(solution)/shard_map/ppermute | solution.py:27
  370.8 39.2 %collective-permute-start.8 = (f32[1,2,256,256]{3,2,1,0:T(8,128)}, f32[1,2,256,256]{3,2,1,0:T(8,128)}, u32[]{:S(2)}, u32[]{:S(2)}) collective-permute-start(f32[1,2,256,256]{3,2,1,0:T(8,128)} %get-tuple-element.2297), channel_id=1, source_target_pairs={{0,8},{8,16},{16,24},{1,9},{9,17},{17,25},{2,10},{10,18},{18,26},{... | collective-permute-start | bytes 1572872 | tf_op jit(solution)/shard_map/ppermute | solution.py:27
  411.9 12.7 %collective-permute-start.9 = (f32[1,2,256,256]{3,2,1,0:T(8,128)}, f32[1,2,256,256]{3,2,1,0:T(8,128)}, u32[]{:S(2)}, u32[]{:S(2)}) collective-permute-start(f32[1,2,256,256]{3,2,1,0:T(8,128)} %get-tuple-element.2299), channel_id=1, source_target_pairs={{0,8},{8,16},{16,24},{1,9},{9,17},{17,25},{2,10},{10,18},{18,26},{... | collective-permute-start | bytes 1572872 | tf_op jit(solution)/shard_map/ppermute | solution.py:27
  442.4 38.0 %collective-permute-start.10 = (f32[1,2,256,256]{3,2,1,0:T(8,128)}, f32[1,2,256,256]{3,2,1,0:T(8,128)}, u32[]{:S(2)}, u32[]{:S(2)}) collective-permute-start(f32[1,2,256,256]{3,2,1,0:T(8,128)} %get-tuple-element.2312), channel_id=1, source_target_pairs={{8,0},{16,8},{24,16},{9,1},{17,9},{25,17},{10,2},{18,10},{26,18},{... | collective-permute-start | bytes 1572872 | tf_op jit(solution)/shard_map/ppermute | solution.py:27
  482.3 12.6 %collective-permute-start.11 = (f32[1,2,256,256]{3,2,1,0:T(8,128)}, f32[1,2,256,256]{3,2,1,0:T(8,128)}, u32[]{:S(2)}, u32[]{:S(2)}) collective-permute-start(f32[1,2,256,256]{3,2,1,0:T(8,128)} %get-tuple-element.2315), channel_id=1, source_target_pairs={{8,0},{16,8},{24,16},{9,1},{17,9},{25,17},{10,2},{18,10},{26,18},{... | collective-permute-start | bytes 1572872 | tf_op jit(solution)/shard_map/ppermute | solution.py:27
  496.7 163.2 %collective-permute-start.12 = (f32[1,2,256,256]{3,2,1,0:T(8,128)}, f32[1,2,256,256]{3,2,1,0:T(8,128)}, u32[]{:S(2)}, u32[]{:S(2)}) collective-permute-start(f32[1,2,256,256]{3,2,1,0:T(8,128)} %get-tuple-element.2318), channel_id=1, source_target_pairs={{8,0},{16,8},{24,16},{9,1},{17,9},{25,17},{10,2},{18,10},{26,18},{... | collective-permute-start | bytes 1572872 | tf_op jit(solution)/shard_map/ppermute | solution.py:27
  699.2 21.5 %collective-permute-start.13 = (f32[1,2,256,256]{3,2,1,0:T(8,128)}, f32[1,2,256,256]{3,2,1,0:T(8,128)}, u32[]{:S(2)}, u32[]{:S(2)}) collective-permute-start(f32[1,2,256,256]{3,2,1,0:T(8,128)} %get-tuple-element.2321), channel_id=1, source_target_pairs={{8,0},{16,8},{24,16},{9,1},{17,9},{25,17},{10,2},{18,10},{26,18},{... | collective-permute-start | bytes 1572872 | tf_op jit(solution)/shard_map/ppermute | solution.py:27
  760.3 18.9 %collective-permute-start.14 = (f32[1,2,256,256]{3,2,1,0:T(8,128)}, f32[1,2,256,256]{3,2,1,0:T(8,128)}, u32[]{:S(2)}, u32[]{:S(2)}) collective-permute-start(f32[1,2,256,256]{3,2,1,0:T(8,128)} %get-tuple-element.2324), channel_id=1, source_target_pairs={{8,0},{16,8},{24,16},{9,1},{17,9},{25,17},{10,2},{18,10},{26,18},{... | collective-permute-start | bytes 1572872 | tf_op jit(solution)/shard_map/ppermute | solution.py:27
  818.7 19.6 %collective-permute-start.15 = (f32[1,2,256,256]{3,2,1,0:T(8,128)}, f32[1,2,256,256]{3,2,1,0:T(8,128)}, u32[]{:S(2)}, u32[]{:S(2)}) collective-permute-start(f32[1,2,256,256]{3,2,1,0:T(8,128)} %get-tuple-element.2327), channel_id=1, source_target_pairs={{8,0},{16,8},{24,16},{9,1},{17,9},{25,17},{10,2},{18,10},{26,18},{... | collective-permute-start | bytes 1572872 | tf_op jit(solution)/shard_map/ppermute | solution.py:27
  878.0 18.5 %collective-permute-start.16 = (f32[1,2,256,256]{3,2,1,0:T(8,128)}, f32[1,2,256,256]{3,2,1,0:T(8,128)}, u32[]{:S(2)}, u32[]{:S(2)}) collective-permute-start(f32[1,2,256,256]{3,2,1,0:T(8,128)} %get-tuple-element.2330), channel_id=1, source_target_pairs={{8,0},{16,8},{24,16},{9,1},{17,9},{25,17},{10,2},{18,10},{26,18},{... | collective-permute-start | bytes 1572872 | tf_op jit(solution)/shard_map/ppermute | solution.py:27
  936.1 19.4 %collective-permute-start.17 = (f32[1,2,256,256]{3,2,1,0:T(8,128)}, f32[1,2,256,256]{3,2,1,0:T(8,128)}, u32[]{:S(2)}, u32[]{:S(2)}) collective-permute-start(f32[1,2,256,256]{3,2,1,0:T(8,128)} %get-tuple-element.2333), channel_id=1, source_target_pairs={{8,0},{16,8},{24,16},{9,1},{17,9},{25,17},{10,2},{18,10},{26,18},{... | collective-permute-start | bytes 1572872 | tf_op jit(solution)/shard_map/ppermute | solution.py:27
  955.5 31.3 %copy-start.18 = (pred[512]{0:T(512)(128)(4,1)S(1)}, pred[512]{0:T(512)(128)(4,1)}, u32[]{:S(2)}) copy-start(pred[512]{0:T(512)(128)(4,1)} %copy-done.17) | copy-start | bytes 1540
  1003.7 83.9 %collective-permute-start.18 = (f32[1,2,4096,128]{3,2,1,0:T(8,128)}, f32[1,2,4096,128]{3,2,1,0:T(8,128)}, u32[]{:S(2)}, u32[]{:S(2)}) collective-permute-start(f32[1,2,4096,128]{3,2,1,0:T(8,128)} %get-tuple-element.2937), channel_id=1, source_target_pairs={{0,1},{1,2},{2,3},{3,4},{4,5},{5,6},{6,7},{8,9},{9,10},{10,11},{11... | collective-permute-start | bytes 12582920 | tf_op jit(solution)/shard_map/ppermute | solution.py:18
  1005.6 86.0 %collective-permute-start.19 = (f32[1,2,4096,128]{3,2,1,0:T(8,128)}, f32[1,2,4096,128]{3,2,1,0:T(8,128)}, u32[]{:S(2)}, u32[]{:S(2)}) collective-permute-start(f32[1,2,4096,128]{3,2,1,0:T(8,128)} %get-tuple-element.2936), channel_id=1, source_target_pairs={{1,0},{2,1},{3,2},{4,3},{5,4},{6,5},{7,6},{9,8},{10,9},{11,10},{12... | collective-permute-start | bytes 12582920 | tf_op jit(solution)/shard_map/ppermute | solution.py:19
  1021.5 66.1 %slice-start = ((f32[1,2,4096,512]{3,2,1,0:T(8,128)}), f32[1,2,4096,256]{3,2,1,0:T(8,128)S(1)}, s32[]{:S(2)}) async-start(f32[1,2,4096,512]{3,2,1,0:T(8,128)} %copy-done), calls=%async_computation | async-start | bytes 16777216 | tf_op jit(solution)/shard_map/slice | solution.py:211
  (6 other events, 28.3 us)
where the time goes:
time: 1120 us; the launch traced here: 1100 us
  waiting for transfers between devices  458 us (41%)
  local copies, waits for them, and re-layouts  234 us (21%)
  matrix products  124 us (11%)
  loops' own time  108 us (10%)
  starting transfers between devices  86.5 us (8%)
  other arithmetic  85.8 us (8%)
    ppermute x16, waiting for transfers between devices, from_behind(): return lax.ppermute(value, axis, pairs)  314 us
    ppermute x2, waiting for transfers between devices, extended(): after = lax.ppermute(initial, axis, down)  79.7 us
    ppermute x16, starting transfers between devices, from_behind(): return lax.ppermute(value, axis, pairs)  71.3 us
    ppermute x2, waiting for transfers between devices, extended(): before = lax.ppermute(last, axis, up)  64.2 us
    dot_general x24, matrix products, transform(): jnp.einsum('ab,pbc->pac', matrix, stacked, precision=lax.Precision.HIGHEST)  63.2 us
    dot_general x24, matrix products, transform(): jnp.einsum('psik,rjsk->prij', halfway, quadrant, precision=lax.Precision....  60.3 us
    another operation x53, local copies, waits for them, and re-layouts  46.4 us
    another operation x9, loops' own time, on_device(): lax.cond(is_valid, run_adjoint, skip_adjoint, grad_ext, fields, inputs, s...  45.9 us
  transfers between devices with their start and end apart: 20, of which 18 were waited for; matrix products, arithmetic and copies ran while one was open for 4% of the time, Pallas kernels for 0%

commit v1 on v0

v1 whole, which is shorter than its diff:
```python
import functools
import math

import jax
import jax.numpy as jnp
from jax import lax
from jax.experimental import pallas as pl
from jax.experimental.pallas import tpu as pltpu
from jax.sharding import PartitionSpec as P

RIM = 128
PAD = 8
MESH = pl.DeviceIdType.MESH
VMEM_LIMIT = 60 * 1024 * 1024


def params(**kw):
    return pltpu.CompilerParams(vmem_limit_bytes=VMEM_LIMIT, **kw)


def vmem():
    return pl.BlockSpec(memory_space=pltpu.VMEM)


def smem():
    return pl.BlockSpec(memory_space=pltpu.SMEM)


def shift(value, axis, by):
    count = lax.axis_size(axis)
    pairs = [(i, i + by) for i in range(count) if 0 <= i + by < count]
    return lax.ppermute(value, axis, pairs)


def make_tables(extent):
    indices = jnp.arange(extent, dtype=jnp.int32)
    product = indices[:, None] * indices[None, :] % extent
    angles = product.astype(jnp.float32) * (2.0 * math.pi / extent)
    cosine = jnp.cos(angles) / math.sqrt(extent)
    sine = jnp.sin(angles) / math.sqrt(extent)

    def split(x):
        hi = lax.reduce_precision(x, 8, 7)
        lo = x - hi
        return hi.astype(jnp.bfloat16), lo.astype(jnp.bfloat16)

    def square(c, s, sign):
        return jnp.concatenate(
            [jnp.concatenate([c, sign * s], 1), jnp.concatenate([-sign * s, c], 1)], 0
        )

    (ch, cl), (sh, sl) = split(cosine), split(sine)
    return (square(ch, sh, 1), square(cl, sl, 1), square(ch, sh, -1), square(cl, sl, -1))


def aligned(row, limit):
    base = jnp.minimum(row // PAD * PAD, limit)
    return pl.multiple_of(base, PAD), row - base


def extract_kernel(own_pos, left_pos, right_pos, trans, own, to_left, to_right,
                   buf_own, buf_left, buf_right, sems):
    slots, _, extent, cols = own.shape
    rows = trans.shape[1]
    tall = extent + PAD
    jobs = (
        (left_pos, buf_left, to_left, 0, RIM),
        (right_pos, buf_right, to_right, cols - RIM, RIM),
        (own_pos, buf_own, own, 0, cols),
    )

    def copy(j, s):
        pos, buf, _, start, width = jobs[j]
        base, off = aligned(pos[s, 0], rows - tall)
        src = trans.at[:, pl.ds(base, tall), pl.ds(start, width)]
        return pltpu.make_async_copy(src, buf.at[s], sems.at[j, s]), off

    for j in range(3):
        for s in range(slots):
            copy(j, s)[0].start()
    for j in range(3):
        _, buf, out, _, _ = jobs[j]

        def body(s, carry):
            one, off = copy(j, s)
            one.wait()
            for p in range(2):
                value = pltpu.roll(buf[s, p], (tall - off) % tall, 0)
                out[s, p] = value[:extent]
            return carry

        lax.fori_loop(0, slots, body, 0)


def keep_columns(shape, tile_at, tiles_total, widths, cols):
    columns = lax.broadcasted_iota(jnp.int32, shape, 1)
    globally = tile_at * cols - RIM + columns
    inside = (globally >= 0) & (globally < tiles_total * cols)
    middle = (columns >= RIM) & (columns < RIM + cols)
    left_ok = (columns < RIM) & (RIM - columns <= widths[0])
    right_ok = (columns >= RIM + cols) & (columns - RIM - cols + 1 <= widths[1])
    return inside & (middle | left_ok | right_ok)


def window_kernel(tiles_total, info, own_pos, left, own, right, out):
    extent, cols = own.shape[-2:]
    wide = cols + 2 * RIM
    s = pl.program_id(0)
    keep = keep_columns((extent, wide), info[2], tiles_total, (info[0], info[1]), cols)
    turn = (wide - own_pos[s, 1]) % wide
    for p in range(2):
        value = jnp.concatenate([left[0, p], own[0, p], right[0, p]], axis=1)
        value = jnp.where(keep, value, 1.0 - p)
        out[0, p] = pltpu.roll(value, turn, 1)[:, :extent]


def unwindow_kernel(tiles_total, info, own_pos, contrib, left, own, right):
    extent, cols = own.shape[-2:]
    wide = cols + 2 * RIM
    s = pl.program_id(0)
    keep = keep_columns((extent, wide), info[2], tiles_total, (info[0], info[1]), cols)
    for p in range(2):
        value = contrib[0, p]
        zeros = jnp.zeros((extent, wide - extent), jnp.float32)
        value = jnp.concatenate([value, zeros], axis=1)
        value = jnp.where(keep, pltpu.roll(value, own_pos[s, 1], 1), 0.0)
        left[0, p] = value[:, :RIM]
        own[0, p] = value[:, RIM : RIM + cols]
        right[0, p] = value[:, RIM + cols :]


def add_rows(out, pos, source, start, width):
    slots, _, extent, _ = source.shape
    rows = out.shape[1]
    tall = extent + PAD

    def body(s, carry):
        base, off = aligned(pos[s, 0], rows - tall)
        for p in range(2):
            value = jnp.concatenate([source[s, p], jnp.zeros((PAD, width), jnp.float32)], axis=0)
            value = pltpu.roll(value, off, 0)
            out[p, pl.ds(base, tall), pl.ds(start, width)] += value
        return carry

    lax.fori_loop(0, slots, body, 0)


def own_grad_kernel(own_pos, own, out):
    out[...] = jnp.zeros(out.shape, out.dtype)
    add_rows(out, own_pos, own, 0, out.shape[2])


def rim_grad_kernel(left_pos, right_pos, from_left, from_right, before, out):
    cols = out.shape[2]
    out[...] = before[...]
    add_rows(out, left_pos, from_left, 0, RIM)
    add_rows(out, right_pos, from_right, cols - RIM, RIM)


def pipeline_kernel(sections, live, windows, probe, phase_kernel, measured,
                    fwd_hi, fwd_lo, inv_hi, inv_lo, adjoint, contrib,
                    arrived, leaving, backed, leaving_back, left_f, left_i, right_f, right_i,
                    tall_b, wide_b, spectrum, send_f, recv_f, send_b, recv_b):
    g = lax.axis_index("cuts")
    last = sections - 1
    slots, _, extent, _ = windows.shape
    two = 2 * extent

    barrier = pltpu.get_barrier_semaphore()

    @pl.when(g > 0)
    def _():
        pl.semaphore_signal(barrier, inc=1, device_id={"cuts": g - 1}, device_id_type=MESH)

    @pl.when(g < last)
    def _():
        pl.semaphore_signal(barrier, inc=1, device_id={"cuts": g + 1}, device_id_type=MESH)

    for table, hi, lo in ((left_f, fwd_hi, fwd_lo), (left_i, inv_hi, inv_lo)):
        table[:, :two] = hi[...]
        table[:, two : 2 * two] = hi[...]
        table[:, 2 * two :] = lo[...]
    for table, hi, lo in ((right_f, inv_hi, inv_lo), (right_i, fwd_hi, fwd_lo)):
        table[:two] = hi[...]
        table[two : 2 * two] = hi[...]
        table[2 * two :] = lo[...]

    inner = (g > 0) & (g < last)

    @pl.when(inner)
    def _():
        pl.semaphore_wait(barrier, 2)

    @pl.when(jnp.logical_not(inner))
    def _():
        pl.semaphore_wait(barrier, 1)

    def put(ref, rows, p, value):
        hi = value.astype(jnp.bfloat16)
        lo = (value - hi.astype(jnp.float32)).astype(jnp.bfloat16)
        n = value.shape[0 if rows else 1]
        for at, part in ((0, hi), (1, lo), (2, hi)):
            place = pl.ds(at * two + p * n, n)
            if rows:
                ref[place, :] = part
            else:
                ref[:, place] = part

    def transform(left, right):
        half = jnp.dot(left[...], tall_b[...], preferred_element_type=jnp.float32)
        put(wide_b, False, 0, half[:extent])
        put(wide_b, False, 1, half[extent:])
        spectrum[...] = jnp.dot(wide_b[...], right[...], preferred_element_type=jnp.float32)

    def times_kernel(sign):
        kr, ki = phase_kernel[0], sign * phase_kernel[1]
        xr, xi = spectrum[:, :extent], spectrum[:, extent:]
        put(tall_b, True, 0, kr * xr - ki * xi)
        put(tall_b, True, 1, kr * xi + ki * xr)

    def propagate(sign):
        transform(left_f, right_f)
        times_kernel(sign)
        transform(left_i, right_i)

    def send_forward(s):
        return pltpu.make_async_remote_copy(
            src_ref=leaving.at[s], dst_ref=arrived.at[s], send_sem=send_f.at[s],
            recv_sem=recv_f.at[s], device_id={"cuts": g + 1}, device_id_type=MESH)

    def send_backward(s):
        return pltpu.make_async_remote_copy(
            src_ref=leaving_back.at[s], dst_ref=backed.at[s], send_sem=send_b.at[s],
            recv_sem=recv_b.at[s], device_id={"cuts": g - 1}, device_id_type=MESH)

    def forward(s):
        @pl.when(g == 0)
        def _():
            arrived[s] = probe[...] * live[s]

        @pl.when(g > 0)
        def _():
            send_forward(s).wait_recv()

        wr, wi = windows[s, 0], windows[s, 1]
        xr, xi = arrived[s, 0], arrived[s, 1]
        put(tall_b, True, 0, wr * xr - wi * xi)
        put(tall_b, True, 1, wr * xi + wi * xr)
        propagate(1.0)

        @pl.when(g < last)
        def _():
            leaving[s, 0] = spectrum[:, :extent]
            leaving[s, 1] = spectrum[:, extent:]
            send_forward(s).start()

    def backward(s):
        @pl.when(g == last)
        def _():
            put(tall_b, True, 0, spectrum[:, :extent])
            put(tall_b, True, 1, spectrum[:, extent:])
            transform(left_f, right_f)
            fr, fi = spectrum[:, :extent], spectrum[:, extent:]
            residual = fr * fr + fi * fi - measured[s].astype(jnp.float32)
            put(tall_b, True, 0, fr * residual)
            put(tall_b, True, 1, fi * residual)
            transform(left_i, right_i)
            put(tall_b, True, 0, spectrum[:, :extent])
            put(tall_b, True, 1, spectrum[:, extent:])

        @pl.when(g < last)
        def _():
            send_backward(s).wait_recv()
            put(tall_b, True, 0, backed[s, 0])
            put(tall_b, True, 1, backed[s, 1])

        propagate(-1.0)
        tr, ti = spectrum[:, :extent], spectrum[:, extent:]
        wr, wi = windows[s, 0], windows[s, 1]
        br, bi = wr * tr + wi * ti, wr * ti - wi * tr

        @pl.when(g > 0)
        def _():
            leaving_back[s, 0] = br
            leaving_back[s, 1] = bi
            send_backward(s).start()

        adjoint[s, 0] = br
        adjoint[s, 1] = bi
        xr, xi = arrived[s, 0], arrived[s, 1]
        contrib[s, 0] = xr * tr + xi * ti
        contrib[s, 1] = xr * ti - xi * tr

    lag = 2 * (last - g)

    def step(k, carry):
        @pl.when(k < slots)
        def _():
            forward(k)

        @pl.when((k >= lag) & (k < lag + slots))
        def _():
            backward(k - lag)

        return carry

    lax.fori_loop(0, slots + 2 * last, step, 0)

    @pl.when(g < last)
    def _():
        lax.fori_loop(0, slots, lambda s, c: (send_forward(s).wait_send(), c)[1], 0)

    @pl.when(g > 0)
    def _():
        lax.fori_loop(0, slots, lambda s, c: (send_backward(s).wait_send(), c)[1], 0)


def on_device(probe_wave, transmission, kernel_phase, measured, counts, positions, widths):
    f32 = jnp.float32
    rows, cols = transmission.shape[2:]
    extent = probe_wave.shape[-1]
    slots = positions.shape[1]
    sections = lax.axis_size("cuts")
    tiles_total = lax.axis_size("tile")
    tile_at = lax.axis_index("tile")
    tall = extent + PAD
    trans = transmission[0]
    own_pos = positions[0]
    right_pos = shift(own_pos, "tile", -1)
    left_pos = shift(own_pos, "tile", 1)
    info = jnp.concatenate([widths[0], tile_at[None].astype(jnp.int32)])
    sds = jax.ShapeDtypeStruct
    wave = sds((slots, 2, extent, extent), f32)
    block = sds((slots, 2, extent, cols), f32)
    rim = sds((slots, 2, extent, RIM), f32)

    own, to_left, to_right = pl.pallas_call(
        extract_kernel,
        out_shape=(block, rim, rim),
        in_specs=[smem(), smem(), smem(), pl.BlockSpec(memory_space=pl.ANY)],
        out_specs=(vmem(), vmem(), vmem()),
        scratch_shapes=[
            pltpu.VMEM((slots, 2, tall, cols), f32),
            pltpu.VMEM((slots, 2, tall, RIM), f32),
            pltpu.VMEM((slots, 2, tall, RIM), f32),
            pltpu.SemaphoreType.DMA((3, slots)),
        ],
        compiler_params=params(),
    )(own_pos, left_pos, right_pos, trans)
    right_rim = shift(to_left, "tile", -1)
    left_rim = shift(to_right, "tile", 1)

    def per_slot(width, height=extent):
        return pl.BlockSpec((1, 2, height, width), lambda s: (s, 0, 0, 0))

    windows = pl.pallas_call(
        functools.partial(window_kernel, tiles_total),
        grid=(slots,),
        out_shape=wave,
        in_specs=[smem(), smem(), per_slot(RIM), per_slot(cols), per_slot(RIM)],
        out_specs=per_slot(extent),
        compiler_params=params(),
    )(info, own_pos, left_rim, own, right_rim)

    tables = make_tables(extent)
    phase_kernel = jnp.stack([jnp.cos(kernel_phase), jnp.sin(kernel_phase)], 0)
    live = (jnp.arange(slots, dtype=jnp.int32) < counts[0]).astype(f32)
    waves = pltpu.VMEM((slots, 2, extent, extent), f32)
    two = 2 * extent
    bf16 = jnp.bfloat16
    adjoint, contrib = pl.pallas_call(
        functools.partial(pipeline_kernel, sections),
        out_shape=(wave, wave),
        in_specs=[smem()] + [vmem()] * 8,
        out_specs=(vmem(), vmem()),
        scratch_shapes=[
            waves, waves, waves, waves,
            pltpu.VMEM((two, 3 * two), bf16),
            pltpu.VMEM((two, 3 * two), bf16),
            pltpu.VMEM((3 * two, two), bf16),
            pltpu.VMEM((3 * two, two), bf16),
            pltpu.VMEM((3 * two, extent), bf16),
            pltpu.VMEM((extent, 3 * two), bf16),
            pltpu.VMEM((extent, two), f32),
            pltpu.SemaphoreType.DMA((slots,)),
            pltpu.SemaphoreType.DMA((slots,)),
            pltpu.SemaphoreType.DMA((slots,)),
            pltpu.SemaphoreType.DMA((slots,)),
        ],
        compiler_params=params(collective_id=0, has_side_effects=True),
    )(live, windows, probe_wave, phase_kernel, measured[0], *tables)

    left_part, own_part, right_part = pl.pallas_call(
        functools.partial(unwindow_kernel, tiles_total),
        grid=(slots,),
        out_shape=(rim, block, rim),
        in_specs=[smem(), smem(), per_slot(extent)],
        out_specs=(per_slot(RIM), per_slot(cols), per_slot(RIM)),
        compiler_params=params(),
    )(info, own_pos, contrib)
    from_right = shift(left_part, "tile", -1)
    from_left = shift(right_part, "tile", 1)
    plane = sds((2, rows, cols), f32)
    grad = pl.pallas_call(
        own_grad_kernel,
        out_shape=plane,
        in_specs=[smem(), vmem()],
        out_specs=vmem(),
        compiler_params=params(),
    )(own_pos, own_part)
    grad = pl.pallas_call(
        rim_grad_kernel,
        out_shape=plane,
        in_specs=[smem(), smem(), vmem(), vmem(), vmem()],
        out_specs=vmem(),
        compiler_params=params(),
    )(left_pos, right_pos, from_left, from_right, grad)
    return (adjoint[None, None], grad[None])


def solution(mesh):
    return jax.shard_map(
        on_device,
        mesh=mesh,
        in_specs=(
            P(),
            P("cuts", None, None, "tile"),
            P(),
            P("tile", None, None, None),
            P("tile"),
            P("tile", None, None),
            P("tile", None),
        ),
        out_specs=(P("cuts", "tile", None, None, None, None), P("cuts", None, None, "tile")),
        check_vma=False,
    )
```

time: 1120 us -> 285 us (0.25); the launches traced: 1100 us -> 283 us
  waiting for transfers between devices: 458 us -> 47.7 us
  local copies, waits for them, and re-layouts: 234 us -> 5.14 us
  Pallas kernels: 0 us -> 191 us
  matrix products: 124 us -> 0 us
  loops' own time: 108 us -> 0 us
  other arithmetic: 85.8 us -> 8.43 us
  starting transfers between devices: 86.5 us -> 29 us
    ppermute x20 -> x6, waiting for transfers between devices: 458 us -> 47.7 us  [shift(): return lax.ppermute(value, axis, pairs)]
    pallas_call x0 -> x6, Pallas kernels: none -> 191 us  [the longest x1 155 us: on_device(): pl.pallas_call(functools.partial(pipeline_kernel, sections), out_shape=(w...]
    dot_general x48 -> x0, matrix products: 124 us -> none  [the longest x24 63.2 us: transform(): jnp.einsum('ab,pbc->pac', matrix, stacked, precision=lax.Precision.HIGHEST)]
    another operation x27 -> x0, loops' own time: 108 us -> none  [the longest x9 45.9 us: on_device(): lax.cond(is_valid, run_adjoint, skip_adjoint, grad_ext, fields, inputs, s...]
    ppermute x20 -> x6, starting transfers between devices: 86.5 us -> 29 us  [shift(): return lax.ppermute(value, axis, pairs)]
    another operation x54 -> x1, local copies, waits for them, and re-layouts: 48.2 us -> 0.97 us  [on_device(): phase_kernel = jnp.stack([jnp.cos(kernel_phase), jnp.sin(kernel_phase)], 0)]
    scatter x6 -> x0, local copies, waits for them, and re-layouts: 39.9 us -> none  [run_adjoint(): grad_ext = grad_ext.at[slice_at].set(grad_plane)]
    reshape x24 -> x0, local copies, waits for them, and re-layouts: 38 us -> none  [transform(): quadrant = matrix.reshape(2, extent, 2, extent)]
  transfers between devices with their start and end apart: 20 -> 6, of which waited for: 18 -> 4; matrix products, arithmetic and copies ran while one was open for 4% -> 3% of each run, Pallas kernels for 0% -> 2%
where the time goes in v1:
time: 285 us; the launch traced here: 283 us
  Pallas kernels  191 us (67%)
  waiting for transfers between devices  47.7 us (17%)
  starting transfers between devices  29 us (10%)
  other arithmetic  8.43 us (3%)
  local copies, waits for them, and re-layouts  5.14 us (2%)
    pallas_call x1, Pallas kernels, on_device(): pl.pallas_call(functools.partial(pipeline_kernel, sections), out_shape=(w...  155 us
    ppermute x6, waiting for transfers between devices, shift(): return lax.ppermute(value, axis, pairs)  47.7 us
    ppermute x6, starting transfers between devices, shift(): return lax.ppermute(value, axis, pairs)  29 us
    pallas_call x1, Pallas kernels, on_device(): pl.pallas_call(rim_grad_kernel, out_shape=plane, in_specs=[smem(), smem()...  9.54 us
    pallas_call x1, Pallas kernels, on_device(): pl.pallas_call(extract_kernel, out_shape=(block, rim, rim), in_specs=[sme...  7.04 us
    pallas_call x1, Pallas kernels, on_device(): pl.pallas_call(own_grad_kernel, out_shape=plane, in_specs=[smem(), vmem()...  6.96 us
    pallas_call x1, Pallas kernels, on_device(): pl.pallas_call(functools.partial(window_kernel, tiles_total), grid=(slots...  6.72 us
    pallas_call x1, Pallas kernels, on_device(): pl.pallas_call(functools.partial(unwindow_kernel, tiles_total), grid=(slo...  6.58 us
  transfers between devices with their start and end apart: 6, of which 4 were waited for; matrix products, arithmetic and copies ran while one was open for 3% of the time, Pallas kernels for 2%

profile of v1, /device:TPU:3, one launch (start us, length us, event | category | flops | bytes accessed | tf_op | source)
XLA Modules:
  0.0 283.2 jit_solution(13488719492955891768)
XLA Ops:
  0.6 0.8 copy.12.own_pos
  1.4 2.6 collective-permute-start.1
  4.0 3.9 %collective-permute-start = (s32[6,2]{1,0:T(8,128)S(1)}, s32[6,2]{1,0:T(8,128)S(1)}, u32[]{:S(2)}, u32[]{:S(2)}) collective-permute-start(s32[6,2]{1,0:T(8,128)S(1)} %copy.12.own_pos), channel_id=1, source_target_pairs={{0,1},{1,2},{2,3},{3,4},{4,5},{5,6},{6,7},{8,9},{9,10},{10,11},{11... | collective-permute-start | bytes 152 | tf_op jit(solution)/shard_map/ppermute | solution.py:32
  7.9 0.0 collective-permute-done.1.right_pos
  7.9 0.7 collective-permute-done.left_pos
  8.6 0.6 copy-done.6
  9.2 7.0 %shard_map.86 = (f32[6,2,256,256]{3,2,1,0:T(8,128)}, f32[6,2,256,128]{3,2,1,0:T(8,128)}, f32[6,2,256,128]{3,2,1,0:T(8,128)}) custom-call(s32[6,2]{1,0:T(8,128)} %copy-done.4, s32[6,2]{1,0:T(8,128)} %copy-done.6, s32[6,2]{1,0:T(8,128)} %copy-done.5, f32[2,4096,256]{2,1,0:T(8,128)} %bitcast.13), custom_call_target="tpu_custom_call" | custom-call | tf_op jit(solution)/shard_map/pallas_call | solution.py:337
  16.2 5.1 %collective-permute-start.2 = (f32[6,2,256,128]{3,2,1,0:T(8,128)}, f32[6,2,256,128]{3,2,1,0:T(8,128)S(1)}, u32[]{:S(2)}, u32[]{:S(2)}) collective-permute-start(f32[6,2,256,128]{3,2,1,0:T(8,128)} %get-tuple-element.10), channel_id=1, source_target_pairs={{0,1},{1,2},{2,3},{3,4},{4,5},{5,6},{6,7},{8,9},{9,10},{10,11},{11... | collective-permute-start | bytes 4718600 | tf_op jit(solution)/shard_map/ppermute | solution.py:32
  21.3 1.9 collective-permute-start.3
  23.9 0.5 compare_convert_fusion.live
  24.4 0.7 pad_add_fusion.info
  25.1 1.0 broadcast_multiply_fusion.1
  26.1 1.0 broadcast_multiply_fusion
  27.1 1.1 fusion.4
  28.3 1.1 reduce-precision_convert_fusion
  29.4 1.0 cosine_bitcast_fusion
  30.4 0.8 pad_maximum_fusion.8.phase_kernel
  31.2 1.1 fusion.3
  32.3 1.1 fusion.1
  33.3 21.5 %collective-permute-done.2.left = f32[6,2,256,128]{3,2,1,0:T(8,128)S(1)} collective-permute-done((f32[6,2,256,128]{3,2,1,0:T(8,128)}, f32[6,2,256,128]{3,2,1,0:T(8,128)S(1)}, u32[]{:S(2)}, u32[]{:S(2)}) %collective-permute-start.2) | collective-permute-done | bytes 1572896 | tf_op jit(solution)/shard_map/ppermute | solution.py:32
  54.9 0.8 collective-permute-done.3.right
  55.6 0.4 copy-done.1
  56.0 0.8 copy-done.2
  56.8 6.7 %shard_map.87.windows = f32[6,2,256,256]{3,2,1,0:T(8,128)} custom-call(s32[3]{0:T(128)} %pad_add_fusion.info, s32[6,2]{1,0:T(8,128)} %copy-done.4, f32[6,2,256,128]{3,2,1,0:T(8,128)} %copy-done.1, f32[6,2,256,256]{3,2,1,0:T(8,128)} %get-tuple-element.11.own, f32[6,2,256,128]{3,2,1,0:T(8,128)} %copy-done.2), custom_call_target="tpu_custom_call" | custom-call | tf_op jit(solution)/shard_map/pallas_call | solution.py:356
  63.5 154.6 %shard_map.88 = (f32[6,2,256,256]{3,2,1,0:T(8,128)}, f32[6,2,256,256]{3,2,1,0:T(8,128)}) custom-call(f32[6]{0:T(128)} %compare_convert_fusion.live, f32[6,2,256,256]{3,2,1,0:T(8,128)} %shard_map.87.windows, f32[2,256,256]{2,1,0:T(8,128)} %probe.1, f32[2,256,256]{2,1,0:T(8,128)} %pad_maximum_fusion.8.phase_kernel, bf16[6,256,256]{2,1,0:T(8,128)(2,1)} %bitcast.16, ...), custom_call_target="tpu_custom_call" | custom-call | tf_op jit(solution)/shard_map/pallas_call | solution.py:371
  218.1 6.6 %shard_map.89 = (f32[6,2,256,128]{3,2,1,0:T(8,128)}, f32[6,2,256,256]{3,2,1,0:T(8,128)}, f32[6,2,256,128]{3,2,1,0:T(8,128)}) custom-call(s32[3]{0:T(128)} %pad_add_fusion.info, s32[6,2]{1,0:T(8,128)} %copy-done.4, f32[6,2,256,256]{3,2,1,0:T(8,128)} %get-tuple-element.14.contrib), custom_call_target="tpu_custom_call" | custom-call | tf_op jit(solution)/shard_map/pallas_call | solution.py:393
  224.7 13.7 %collective-permute-start.4 = (f32[6,2,256,128]{3,2,1,0:T(8,128)}, f32[6,2,256,128]{3,2,1,0:T(8,128)}, u32[]{:S(2)}, u32[]{:S(2)}) collective-permute-start(f32[6,2,256,128]{3,2,1,0:T(8,128)} %get-tuple-element.15), channel_id=1, source_target_pairs={{0,1},{1,2},{2,3},{3,4},{4,5},{5,6},{6,7},{8,9},{9,10},{10,11},{11... | collective-permute-start | bytes 4718600 | tf_op jit(solution)/shard_map/ppermute | solution.py:32
  238.4 1.9 collective-permute-start.5
  240.3 7.0 %shard_map.90.before = f32[2,4096,256]{2,1,0:T(8,128)} custom-call(s32[6,2]{1,0:T(8,128)} %copy-done.4, f32[6,2,256,256]{3,2,1,0:T(8,128)} %get-tuple-element.17.own), custom_call_target="tpu_custom_call" | custom-call | tf_op jit(solution)/shard_map/pallas_call | solution.py:404
  247.3 24.7 %collective-permute-done.4.from_left = f32[6,2,256,128]{3,2,1,0:T(8,128)} collective-permute-done((f32[6,2,256,128]{3,2,1,0:T(8,128)}, f32[6,2,256,128]{3,2,1,0:T(8,128)}, u32[]{:S(2)}, u32[]{:S(2)}) %collective-permute-start.4) | collective-permute-done | bytes 1572896 | tf_op jit(solution)/shard_map/ppermute | solution.py:32
  272.0 9.5 %shard_map.91 = f32[2,4096,256]{2,1,0:T(8,128)} custom-call(s32[6,2]{1,0:T(8,128)} %copy-done.6, s32[6,2]{1,0:T(8,128)} %copy-done.5, f32[6,2,256,128]{3,2,1,0:T(8,128)} %collective-permute-done.4.from_left, f32[6,2,256,128]{3,2,1,0:T(8,128)} %collective-permute-done.5.from_right, f32[2,4096,256]{2,1,0:T(8,128)} %shard_map.90.before), custom_call_target="tpu_custom_call" | custom-call | tf_op jit(solution)/shard_map/pallas_call | solution.py:411
  281.5 1.7 copy.17
  (14 shorter events, 0.0 us)
Async XLA Ops:
  1.4 7.2 %copy-start.4 = (s32[6,2]{1,0:T(8,128)}, s32[6,2]{1,0:T(8,128)S(1)}, u32[]{:S(2)}) copy-start(s32[6,2]{1,0:T(8,128)S(1)} %copy.12.own_pos) | copy-start | bytes 148
  1.4 6.5 %collective-permute-start.1 = (s32[6,2]{1,0:T(8,128)S(1)}, s32[6,2]{1,0:T(8,128)S(1)}, u32[]{:S(2)}, u32[]{:S(2)}) collective-permute-start(s32[6,2]{1,0:T(8,128)S(1)} %copy.12.own_pos), channel_id=1, source_target_pairs={{1,0},{2,1},{3,2},{4,3},{5,4},{6,5},{7,6},{9,8},{10,9},{11,10},{12... | collective-permute-start | bytes 152 | tf_op jit(solution)/shard_map/ppermute | solution.py:32
  4.0 4.6 %collective-permute-start = (s32[6,2]{1,0:T(8,128)S(1)}, s32[6,2]{1,0:T(8,128)S(1)}, u32[]{:S(2)}, u32[]{:S(2)}) collective-permute-start(s32[6,2]{1,0:T(8,128)S(1)} %copy.12.own_pos), channel_id=1, source_target_pairs={{0,1},{1,2},{2,3},{3,4},{4,5},{5,6},{6,7},{8,9},{9,10},{10,11},{11... | collective-permute-start | bytes 152 | tf_op jit(solution)/shard_map/ppermute | solution.py:32
  7.9 0.7 copy-start.5
  8.6 0.6 copy-start.6
  9.2 15.2 %copy-start.7 = (s32[1,2]{1,0:T(1,128)S(1)}, s32[1,2]{1,0:T(1,128)}, u32[]{:S(2)}) copy-start(s32[1,2]{1,0:T(1,128)} %param.13) | copy-start | bytes 28
  9.2 20.2 %copy-start.3 = (f32[256,256]{1,0:T(8,128)S(1)}, f32[256,256]{1,0:T(8,128)}, u32[]{:S(2)}) copy-start(f32[256,256]{1,0:T(8,128)} %param.9) | copy-start | bytes 786436
  16.2 38.6 %collective-permute-start.2 = (f32[6,2,256,128]{3,2,1,0:T(8,128)}, f32[6,2,256,128]{3,2,1,0:T(8,128)S(1)}, u32[]{:S(2)}, u32[]{:S(2)}) collective-permute-start(f32[6,2,256,128]{3,2,1,0:T(8,128)} %get-tuple-element.10), channel_id=1, source_target_pairs={{0,1},{1,2},{2,3},{3,4},{4,5},{5,6},{6,7},{8,9},{9,10},{10,11},{11... | collective-permute-start | bytes 4718600 | tf_op jit(solution)/shard_map/ppermute | solution.py:32
  21.3 34.3 %collective-permute-start.3 = (f32[6,2,256,128]{3,2,1,0:T(8,128)}, f32[6,2,256,128]{3,2,1,0:T(8,128)S(1)}, u32[]{:S(2)}, u32[]{:S(2)}) collective-permute-start(f32[6,2,256,128]{3,2,1,0:T(8,128)} %get-tuple-element.12), channel_id=1, source_target_pairs={{1,0},{2,1},{3,2},{4,3},{5,4},{6,5},{7,6},{9,8},{10,9},{11,10},{12... | collective-permute-start | bytes 4718600 | tf_op jit(solution)/shard_map/ppermute | solution.py:32
  54.9 1.2 copy-start.1
  55.6 1.1 copy-start.2
  224.7 47.3 %collective-permute-start.4 = (f32[6,2,256,128]{3,2,1,0:T(8,128)}, f32[6,2,256,128]{3,2,1,0:T(8,128)}, u32[]{:S(2)}, u32[]{:S(2)}) collective-permute-start(f32[6,2,256,128]{3,2,1,0:T(8,128)} %get-tuple-element.15), channel_id=1, source_target_pairs={{0,1},{1,2},{2,3},{3,4},{4,5},{5,6},{6,7},{8,9},{9,10},{10,11},{11... | collective-permute-start | bytes 4718600 | tf_op jit(solution)/shard_map/ppermute | solution.py:32
  238.4 33.6 %collective-permute-start.5 = (f32[6,2,256,128]{3,2,1,0:T(8,128)}, f32[6,2,256,128]{3,2,1,0:T(8,128)}, u32[]{:S(2)}, u32[]{:S(2)}) collective-permute-start(f32[6,2,256,128]{3,2,1,0:T(8,128)} %get-tuple-element.16), channel_id=1, source_target_pairs={{1,0},{2,1},{3,2},{4,3},{5,4},{6,5},{7,6},{9,8},{10,9},{11,10},{12... | collective-permute-start | bytes 4718600 | tf_op jit(solution)/shard_map/ppermute | solution.py:32
  247.3 34.3 %copy-start = (f32[6,2,256,256]{3,2,1,0:T(8,128)S(1)}, f32[6,2,256,256]{3,2,1,0:T(8,128)}, u32[]{:S(2)}) copy-start(f32[6,2,256,256]{3,2,1,0:T(8,128)} %get-tuple-element.13) | copy-start | bytes 9437188

commit v2 on v1

v2 whole, which is shorter than its diff:
```python
import functools
import math

import jax
import jax.numpy as jnp
from jax import lax
from jax.experimental import pallas as pl
from jax.experimental.pallas import tpu as pltpu
from jax.sharding import PartitionSpec as P

RIM = 128
PAD = 8
MESH = pl.DeviceIdType.MESH
VMEM_LIMIT = 60 * 1024 * 1024


def params(**kw):
    return pltpu.CompilerParams(vmem_limit_bytes=VMEM_LIMIT, **kw)


def vmem():
    return pl.BlockSpec(memory_space=pltpu.VMEM)


def smem():
    return pl.BlockSpec(memory_space=pltpu.SMEM)


def shift(value, axis, by):
    count = lax.axis_size(axis)
    pairs = [(i, i + by) for i in range(count) if 0 <= i + by < count]
    return lax.ppermute(value, axis, pairs)


def make_tables(extent):
    indices = jnp.arange(extent, dtype=jnp.int32)
    product = indices[:, None] * indices[None, :] % extent
    angles = product.astype(jnp.float32) * (2.0 * math.pi / extent)
    cosine = jnp.cos(angles) / math.sqrt(extent)
    sine = jnp.sin(angles) / math.sqrt(extent)

    def split(x):
        hi = lax.reduce_precision(x, 8, 7)
        lo = x - hi
        return hi.astype(jnp.bfloat16), lo.astype(jnp.bfloat16)

    def square(c, s, sign):
        return jnp.concatenate(
            [jnp.concatenate([c, sign * s], 1), jnp.concatenate([-sign * s, c], 1)], 0
        )

    (ch, cl), (sh, sl) = split(cosine), split(sine)
    return (square(ch, sh, 1), square(cl, sl, 1), square(ch, sh, -1), square(cl, sl, -1))


def aligned(row, limit):
    base = jnp.minimum(row // PAD * PAD, limit)
    return pl.multiple_of(base, PAD), row - base


def extract_kernel(here, left_pos, right_pos, own_pos, trans, own, to_left, to_right,
                   buf_own, buf_left, buf_right, sems):
    slots, _, extent, _ = own.shape
    rows, cols = trans.shape[1:]
    tall = extent + PAD
    slack = cols + 2 * RIM - extent
    jobs = (
        (left_pos, buf_left, 0, RIM),
        (right_pos, buf_right, cols - RIM, RIM),
        (own_pos, buf_own, 0, cols),
    )

    def copy(j, s):
        pos, buf, start, width = jobs[j]
        base, off = aligned(pos[s, 0], rows - tall)
        src = trans.at[:, pl.ds(base, tall), pl.ds(start, width)]
        return pltpu.make_async_copy(src, buf.at[s], sems.at[j, s]), off

    for j in range(3):
        for s in range(slots):
            copy(j, s)[0].start()

    def columns(width):
        return lax.broadcasted_iota(jnp.int32, (extent, width), 1)

    def load(j, s, p, off, turn):
        value = pltpu.roll(jobs[j][1][s, p], (tall - off) % tall, 0)[:extent]
        return pltpu.roll(value, turn, 1)

    def for_left(s, carry):
        one, off = copy(0, s)
        one.wait()
        short = slack - left_pos[s, 1]
        at = columns(RIM) - short
        good = (at >= 0) & (at + 1 <= left_pos[slots, 1])
        for p in range(2):
            value = load(0, s, p, off, short % RIM)
            to_left[s, p] = jnp.where(good, value, 0.0)
        return carry

    def for_right(s, carry):
        one, off = copy(1, s)
        one.wait()
        col = right_pos[s, 1]
        at = columns(RIM) + col
        good = (at < RIM) & (RIM - at <= right_pos[slots, 0])
        for p in range(2):
            value = load(1, s, p, off, (cols - col) % RIM)
            to_right[s, p] = jnp.where(good, value, 0.0)
        return carry

    def for_own(s, carry):
        one, off = copy(2, s)
        one.wait()
        col = own_pos[s, 1]
        at = columns(extent) + col
        middle = (at >= RIM) & (at < RIM + cols)
        left_ok = (here[0] > 0) & (at < RIM) & (RIM - at <= own_pos[slots, 0])
        right_ok = (here[0] < here[1] - 1) & (at >= RIM + cols) & (
            at - RIM - cols + 1 <= own_pos[slots, 1])
        rim = left_ok | right_ok
        for p in range(2):
            value = load(2, s, p, off, (cols + RIM - col) % cols)
            out = jnp.where(rim, 0.0, 1.0 - p)
            own[s, p] = jnp.where(middle, value, out)
        return carry

    lax.fori_loop(0, slots, for_left, 0)
    lax.fori_loop(0, slots, for_right, 0)
    lax.fori_loop(0, slots, for_own, 0)


def gather_kernel(left_pos, right_pos, own_pos, contrib, from_left, from_right, out):
    slots, _, extent, _ = contrib.shape
    rows, cols = out.shape[1:]
    tall = extent + PAD
    slack = cols + 2 * RIM - extent
    out[...] = jnp.zeros(out.shape, out.dtype)

    def columns(width):
        return lax.broadcasted_iota(jnp.int32, (extent, width), 1)

    def add(source, s, pos, good, turn, start, width):
        base, off = aligned(pos[s, 0], rows - tall)
        for p in range(2):
            value = jnp.where(good, pltpu.roll(source[s, p], turn, 1), 0.0)
            value = jnp.concatenate([value, jnp.zeros((PAD, width), jnp.float32)], axis=0)
            value = pltpu.roll(value, off, 0)
            out[p, pl.ds(base, tall), pl.ds(start, width)] += value

    def body(s, carry):
        col = own_pos[s, 1]
        at = columns(cols) + RIM - col
        good = (at >= 0) & (at < extent)
        add(contrib, s, own_pos, good, (col + cols - RIM) % cols, 0, cols)
        short = slack - left_pos[s, 1]
        at = columns(RIM)
        good = (at + short < RIM) & (at + 1 <= left_pos[slots, 1])
        add(from_left, s, left_pos, good, (cols - short) % RIM, 0, RIM)
        col = right_pos[s, 1]
        good = (at >= col) & (RIM - at <= right_pos[slots, 0])
        add(from_right, s, right_pos, good, col % RIM, cols - RIM, RIM)
        return carry

    lax.fori_loop(0, slots, body, 0)


def pipeline_kernel(sections, tiles, live, to_left, to_right, own, probe, phase_kernel, measured,
                    fwd_hi, fwd_lo, inv_hi, inv_lo, adjoint, contrib, from_left, from_right,
                    windows, left_rim, right_rim, got_left, got_right,
                    arrived, leaving, backed, left_f, left_i, right_f, right_i,
                    tall_b, wide_b, spectrum, send_f, recv_f, send_b, recv_b,
                    send_rim, recv_rim, send_got, recv_got):
    g = lax.axis_index("cuts")
    t = lax.axis_index("tile")
    last = sections - 1
    end = tiles - 1
    slots, _, extent, _ = own.shape
    two = 2 * extent

    barrier = pltpu.get_barrier_semaphore()

    @pl.when(g > 0)
    def _():
        pl.semaphore_signal(barrier, inc=1, device_id={"cuts": g - 1}, device_id_type=MESH)

    @pl.when(g < last)
    def _():
        pl.semaphore_signal(barrier, inc=1, device_id={"cuts": g + 1}, device_id_type=MESH)

    @pl.when(t > 0)
    def _():
        pl.semaphore_signal(barrier, inc=1, device_id={"tile": t - 1}, device_id_type=MESH)

    @pl.when(t < end)
    def _():
        pl.semaphore_signal(barrier, inc=1, device_id={"tile": t + 1}, device_id_type=MESH)

    for table, hi, lo in ((left_f, fwd_hi, fwd_lo), (left_i, inv_hi, inv_lo)):
        table[:, :two] = hi[...]
        table[:, two : 2 * two] = hi[...]
        table[:, 2 * two :] = lo[...]
    for table, hi, lo in ((right_f, inv_hi, inv_lo), (right_i, fwd_hi, fwd_lo)):
        table[:two] = hi[...]
        table[two : 2 * two] = hi[...]
        table[2 * two :] = lo[...]

    peers = (g + last - 1) // last + 1 - g // last + (t + end - 1) // end + 1 - t // end
    pl.semaphore_wait(barrier, peers)

    def rim_copy(side, s):
        src, dst = ((to_left, right_rim), (to_right, left_rim))[side]
        return pltpu.make_async_remote_copy(
            src_ref=src.at[s], dst_ref=dst.at[s], send_sem=send_rim.at[side, s],
            recv_sem=recv_rim.at[side, s], device_id={"tile": t + (-1, 1)[side]},
            device_id_type=MESH)

    def got_copy(side, s):
        start, dst = ((0, got_right), (extent - RIM, got_left))[side]
        return pltpu.make_async_remote_copy(
            src_ref=contrib.at[s, :, :, pl.ds(start, RIM)], dst_ref=dst.at[s],
            send_sem=send_got.at[side, s], recv_sem=recv_got.at[side, s],
            device_id={"tile": t + (-1, 1)[side]}, device_id_type=MESH)

    def each(action):
        def body(s, carry):
            action(s)
            return carry

        lax.fori_loop(0, slots, body, 0)

    @pl.when(t > 0)
    def _():
        each(lambda s: rim_copy(0, s).start())

    @pl.when(t < end)
    def _():
        each(lambda s: rim_copy(1, s).start())

    @pl.when(t == 0)
    def _():
        left_rim[...] = jnp.zeros(left_rim.shape, left_rim.dtype)
        got_left[...] = jnp.zeros(got_left.shape, got_left.dtype)

    @pl.when(t == end)
    def _():
        right_rim[...] = jnp.zeros(right_rim.shape, right_rim.dtype)
        got_right[...] = jnp.zeros(got_right.shape, got_right.dtype)

    def put(ref, rows, p, value):
        hi = value.astype(jnp.bfloat16)
        lo = (value - hi.astype(jnp.float32)).astype(jnp.bfloat16)
        n = value.shape[0 if rows else 1]
        for at, part in ((0, hi), (1, lo), (2, hi)):
            place = pl.ds(at * two + p * n, n)
            if rows:
                ref[place, :] = part
            else:
                ref[:, place] = part

    def transform(left, right):
        half = jnp.dot(left[...], tall_b[...], preferred_element_type=jnp.float32)
        put(wide_b, False, 0, half[:extent])
        put(wide_b, False, 1, half[extent:])
        spectrum[...] = jnp.dot(wide_b[...], right[...], preferred_element_type=jnp.float32)

    def times_kernel(sign):
        kr, ki = phase_kernel[0], sign * phase_kernel[1]
        xr, xi = spectrum[:, :extent], spectrum[:, extent:]
        put(tall_b, True, 0, kr * xr - ki * xi)
        put(tall_b, True, 1, kr * xi + ki * xr)

    def propagate(sign):
        transform(left_f, right_f)
        times_kernel(sign)
        transform(left_i, right_i)

    def send_forward(s):
        return pltpu.make_async_remote_copy(
            src_ref=leaving.at[s], dst_ref=arrived.at[s], send_sem=send_f.at[s],
            recv_sem=recv_f.at[s], device_id={"cuts": g + 1}, device_id_type=MESH)

    def send_backward(s):
        return pltpu.make_async_remote_copy(
            src_ref=adjoint.at[s], dst_ref=backed.at[s], send_sem=send_b.at[s],
            recv_sem=recv_b.at[s], device_id={"cuts": g - 1}, device_id_type=MESH)

    def forward(s):
        @pl.when(g == 0)
        def _():
            arrived[s] = probe[...] * live[s]

        @pl.when(g > 0)
        def _():
            send_forward(s).wait_recv()

        @pl.when(t < end)
        def _():
            rim_copy(0, s).wait_recv()

        @pl.when(t > 0)
        def _():
            rim_copy(1, s).wait_recv()

        for p in range(2):
            windows[s, p, :, :RIM] = own[s, p, :, :RIM] + left_rim[s, p]
            if extent > 2 * RIM:
                windows[s, p, :, RIM : extent - RIM] = own[s, p, :, RIM : extent - RIM]
            windows[s, p, :, extent - RIM :] = own[s, p, :, extent - RIM :] + right_rim[s, p]
        wr, wi = windows[s, 0], windows[s, 1]
        xr, xi = arrived[s, 0], arrived[s, 1]
        put(tall_b, True, 0, wr * xr - wi * xi)
        put(tall_b, True, 1, wr * xi + wi * xr)
        propagate(1.0)

        @pl.when(g < last)
        def _():
            leaving[s, 0] = spectrum[:, :extent]
            leaving[s, 1] = spectrum[:, extent:]
            send_forward(s).start()

    def backward(s):
        @pl.when(g == last)
        def _():
            put(tall_b, True, 0, spectrum[:, :extent])
            put(tall_b, True, 1, spectrum[:, extent:])
            transform(left_f, right_f)
            fr, fi = spectrum[:, :extent], spectrum[:, extent:]
            residual = fr * fr + fi * fi - measured[s].astype(jnp.float32)
            put(tall_b, True, 0, fr * residual)
            put(tall_b, True, 1, fi * residual)
            transform(left_i, right_i)
            put(tall_b, True, 0, spectrum[:, :extent])
            put(tall_b, True, 1, spectrum[:, extent:])

        @pl.when(g < last)
        def _():
            send_backward(s).wait_recv()
            put(tall_b, True, 0, backed[s, 0])
            put(tall_b, True, 1, backed[s, 1])

        propagate(-1.0)
        tr, ti = spectrum[:, :extent], spectrum[:, extent:]
        wr, wi = windows[s, 0], windows[s, 1]
        br, bi = wr * tr + wi * ti, wr * ti - wi * tr

        adjoint[s, 0] = br
        adjoint[s, 1] = bi

        @pl.when(g > 0)
        def _():
            send_backward(s).start()

        xr, xi = arrived[s, 0], arrived[s, 1]
        contrib[s, 0] = xr * tr + xi * ti
        contrib[s, 1] = xr * ti - xi * tr

        @pl.when(t > 0)
        def _():
            got_copy(0, s).start()

        @pl.when(t < end)
        def _():
            got_copy(1, s).start()

    lag = 2 * (last - g)

    def step(k, carry):
        @pl.when(k < slots)
        def _():
            forward(k)

        @pl.when((k >= lag) & (k < lag + slots))
        def _():
            backward(k - lag)

        return carry

    lax.fori_loop(0, slots + 2 * last, step, 0)

    @pl.when(g < last)
    def _():
        each(lambda s: send_forward(s).wait_send())

    @pl.when(g > 0)
    def _():
        each(lambda s: send_backward(s).wait_send())

    @pl.when(t < end)
    def _():
        each(lambda s: got_copy(0, s).wait_recv())

    @pl.when(t > 0)
    def _():
        each(lambda s: got_copy(1, s).wait_recv())

    def finish(side):
        def body(s):
            rim_copy(side, s).wait_send()
            got_copy(side, s).wait_send()

        each(body)

    @pl.when(t > 0)
    def _():
        finish(0)

    @pl.when(t < end)
    def _():
        finish(1)

    from_left[...] = got_left[...]
    from_right[...] = got_right[...]


def on_device(probe_wave, transmission, kernel_phase, measured, counts, positions, widths):
    f32 = jnp.float32
    rows, cols = transmission.shape[2:]
    extent = probe_wave.shape[-1]
    slots = positions.shape[1]
    sections = lax.axis_size("cuts")
    tiles_total = lax.axis_size("tile")
    tile_at = lax.axis_index("tile")
    tall = extent + PAD
    trans = transmission[0]
    own_pos = jnp.concatenate([positions[0], widths], 0)
    right_pos = shift(own_pos, "tile", -1)
    left_pos = shift(own_pos, "tile", 1)
    here = jnp.stack([tile_at, jnp.asarray(tiles_total, tile_at.dtype)]).astype(jnp.int32)
    sds = jax.ShapeDtypeStruct
    wave = sds((slots, 2, extent, extent), f32)
    rim = sds((slots, 2, extent, RIM), f32)
    assert extent == cols and extent >= 2 * RIM

    own, to_left, to_right = pl.pallas_call(
        extract_kernel,
        out_shape=(wave, rim, rim),
        in_specs=[smem()] * 4 + [pl.BlockSpec(memory_space=pl.ANY)],
        out_specs=(vmem(), vmem(), vmem()),
        scratch_shapes=[
            pltpu.VMEM((slots, 2, tall, cols), f32),
            pltpu.VMEM((slots, 2, tall, RIM), f32),
            pltpu.VMEM((slots, 2, tall, RIM), f32),
            pltpu.SemaphoreType.DMA((3, slots)),
        ],
        compiler_params=params(),
    )(here, left_pos, right_pos, own_pos, trans)

    tables = make_tables(extent)
    phase_kernel = jnp.stack([jnp.cos(kernel_phase), jnp.sin(kernel_phase)], 0)
    live = (jnp.arange(slots, dtype=jnp.int32) < counts[0]).astype(f32)
    waves = pltpu.VMEM((slots, 2, extent, extent), f32)
    two = 2 * extent
    bf16 = jnp.bfloat16
    rims = pltpu.VMEM((slots, 2, extent, RIM), f32)
    adjoint, contrib, from_left, from_right = pl.pallas_call(
        functools.partial(pipeline_kernel, sections, tiles_total),
        out_shape=(wave, wave, rim, rim),
        in_specs=[smem()] + [vmem()] * 10,
        out_specs=(vmem(),) * 4,
        scratch_shapes=[
            waves, rims, rims, rims, rims,
            waves, waves, waves,
            pltpu.VMEM((two, 3 * two), bf16),
            pltpu.VMEM((two, 3 * two), bf16),
            pltpu.VMEM((3 * two, two), bf16),
            pltpu.VMEM((3 * two, two), bf16),
            pltpu.VMEM((3 * two, extent), bf16),
            pltpu.VMEM((extent, 3 * two), bf16),
            pltpu.VMEM((extent, two), f32),
            pltpu.SemaphoreType.DMA((slots,)),
            pltpu.SemaphoreType.DMA((slots,)),
            pltpu.SemaphoreType.DMA((slots,)),
            pltpu.SemaphoreType.DMA((slots,)),
            pltpu.SemaphoreType.DMA((2, slots)),
            pltpu.SemaphoreType.DMA((2, slots)),
            pltpu.SemaphoreType.DMA((2, slots)),
            pltpu.SemaphoreType.DMA((2, slots)),
        ],
        compiler_params=params(collective_id=0, has_side_effects=True),
    )(live, to_left, to_right, own, probe_wave, phase_kernel, measured[0], *tables)

    grad = pl.pallas_call(
        gather_kernel,
        out_shape=sds((2, rows, cols), f32),
        in_specs=[smem()] * 3 + [vmem()] * 3,
        out_specs=vmem(),
        compiler_params=params(),
    )(left_pos, right_pos, own_pos, contrib, from_left, from_right)
    return (adjoint[None, None], grad[None])


def solution(mesh):
    return jax.shard_map(
        on_device,
        mesh=mesh,
        in_specs=(
            P(),
            P("cuts", None, None, "tile"),
            P(),
            P("tile", None, None, None),
            P("tile"),
            P("tile", None, None),
            P("tile", None),
        ),
        out_specs=(P("cuts", "tile", None, None, None, None), P("cuts", None, None, "tile")),
        check_vma=False,
    )
```

time: 285 us -> 234 us (0.82)
  waiting for transfers between devices: 47.7 us -> 0.01 us
  starting transfers between devices: 29 us -> 6.46 us
  Pallas kernels: 191 us -> 212 us
    ppermute x6 -> x2, waiting for transfers between devices: 47.7 us -> 0.01 us  [shift(): return lax.ppermute(value, axis, pairs)]
    ppermute x6 -> x2, starting transfers between devices: 29 us -> 6.46 us  [shift(): return lax.ppermute(value, axis, pairs)]
    pallas_call x6 -> x3, Pallas kernels: 191 us -> 212 us  [the longest x1 193 us: on_device(): pl.pallas_call(functools.partial(pipeline_kernel, sections, tiles_total),...]
  transfers between devices with their start and end apart: 6 -> 2, of which waited for: 4 -> 0; matrix products, arithmetic and copies ran while one was open for 3% -> 4% of each run, Pallas kernels for 2% -> 0%
where the time goes in v2:
time: 234 us; the launch traced here: 233 us
  Pallas kernels  212 us (91%)
  other arithmetic  9.11 us (4%)
  starting transfers between devices  6.46 us (3%)
  local copies, waits for them, and re-layouts  4.87 us (2%)
    pallas_call x1, Pallas kernels, on_device(): pl.pallas_call(functools.partial(pipeline_kernel, sections, tiles_total),...  193 us
    pallas_call x1, Pallas kernels, on_device(): pl.pallas_call(gather_kernel, out_shape=sds((2, rows, cols), f32), in_spe...  10.4 us
    pallas_call x1, Pallas kernels, on_device(): pl.pallas_call(extract_kernel, out_shape=(wave, rim, rim), in_specs=[smem...  8.66 us
    ppermute x2, starting transfers between devices, shift(): return lax.ppermute(value, axis, pairs)  6.46 us
  transfers between devices with their start and end apart: 2, of which 0 were waited for; matrix products, arithmetic and copies ran while one was open for 4% of the time, Pallas kernels for 0%

profile of v2, /device:TPU:3, one launch (start us, length us, event | category | flops | bytes accessed | tf_op | source)
XLA Modules:
  0.0 233.5 jit_solution(9667057753601658232)
XLA Ops:
  0.6 0.8 copy.15
  1.4 0.7 pad_add_fusion.own_pos
  2.1 0.0 copy-start.1
  2.1 2.6 %collective-permute-start.1 = (s32[7,2]{1,0:T(8,128)S(1)}, s32[7,2]{1,0:T(8,128)S(1)}, u32[]{:S(2)}, u32[]{:S(2)}) collective-permute-start(s32[7,2]{1,0:T(8,128)S(1)} %pad_add_fusion.own_pos), channel_id=1, source_target_pairs={{1,0},{2,1},{3,2},{4,3},{5,4},{6,5},{7,6},{9,8},{10,9},{11,10},{12... | collective-permute-start | bytes 176 | tf_op jit(solution)/shard_map/ppermute | solution.py:32
  4.6 3.9 %collective-permute-start = (s32[7,2]{1,0:T(8,128)S(1)}, s32[7,2]{1,0:T(8,128)S(1)}, u32[]{:S(2)}, u32[]{:S(2)}) collective-permute-start(s32[7,2]{1,0:T(8,128)S(1)} %pad_add_fusion.own_pos), channel_id=1, source_target_pairs={{0,1},{1,2},{2,3},{3,4},{4,5},{5,6},{6,7},{8,9},{9,10},{10,11},{11... | collective-permute-start | bytes 176 | tf_op jit(solution)/shard_map/ppermute | solution.py:32
  8.5 1.0 broadcast_multiply_fusion.1
  9.5 1.0 broadcast_multiply_fusion
  10.6 1.1 fusion.4
  11.7 1.1 reduce-precision_convert_fusion
  13.5 0.5 compare_convert_fusion.live
  14.0 1.9 cosine_bitcast_fusion
  15.9 0.8 pad_maximum_fusion.8.phase_kernel
  16.7 1.1 fusion.3
  17.8 1.1 fusion.1
  18.9 0.6 pad_add_fusion.1.here
  19.5 0.0 collective-permute-done.1.right_pos
  19.5 0.0 copy-start.2
  19.5 0.0 collective-permute-done.left_pos
  19.5 0.0 copy-start.3
  19.5 0.0 copy-done.1
  19.5 0.6 copy-done.2
  20.1 0.0 copy-done.3
  20.1 8.7 %shard_map.86 = (f32[6,2,256,256]{3,2,1,0:T(8,128)}, f32[6,2,256,128]{3,2,1,0:T(8,128)}, f32[6,2,256,128]{3,2,1,0:T(8,128)}) custom-call(s32[2]{0:T(128)} %pad_add_fusion.1.here, s32[7,2]{1,0:T(8,128)} %copy-done.3, s32[7,2]{1,0:T(8,128)} %copy-done.2, s32[7,2]{1,0:T(8,128)} %copy-done.1, f32[2,4096,256]{2,1,0:T(8,128)} %bitcast.12), custom_call_target="tpu_custom_call" | custom-call | tf_op jit(solution)/shard_map/pallas_call | solution.py:435
  28.8 192.6 %shard_map.87 = (f32[6,2,256,256]{3,2,1,0:T(8,128)}, f32[6,2,256,256]{3,2,1,0:T(8,128)}, f32[6,2,256,128]{3,2,1,0:T(8,128)}, f32[6,2,256,128]{3,2,1,0:T(8,128)}) custom-call(f32[6]{0:T(128)} %compare_convert_fusion.live, f32[6,2,256,128]{3,2,1,0:T(8,128)} %get-tuple-element.9.to_left, f32[6,2,256,128]{3,2,1,0:T(8,128)} %get-tuple-element.10.to_right, ...), custom_call_target="tpu_custom_call" | custom-call | tf_op jit(solution)/shard_map/pallas_call | solution.py:456
  221.4 0.0 copy-start
  221.4 10.4 %shard_map.88 = f32[2,4096,256]{2,1,0:T(8,128)} custom-call(s32[7,2]{1,0:T(8,128)} %copy-done.3, s32[7,2]{1,0:T(8,128)} %copy-done.2, s32[7,2]{1,0:T(8,128)} %copy-done.1, f32[6,2,256,256]{3,2,1,0:T(8,128)} %get-tuple-element.13.contrib, f32[6,2,256,128]{3,2,1,0:T(8,128)} %get-tuple-element.14.from_left, f32[6,2,256,128]{3,2,1,0:T(8,128)} %get-tuple-element.15.from_right), custom_call_target="tpu_custom_call" | custom-call | tf_op jit(solution)/shard_map/pallas_call | solution.py:483
  231.8 0.0 copy-done
  231.8 1.7 copy.18
Async XLA Ops:
  2.1 17.5 %copy-start.1 = (s32[7,2]{1,0:T(8,128)}, s32[7,2]{1,0:T(8,128)S(1)}, u32[]{:S(2)}) copy-start(s32[7,2]{1,0:T(8,128)S(1)} %pad_add_fusion.own_pos) | copy-start | bytes 172
  2.1 17.5 %collective-permute-start.1 = (s32[7,2]{1,0:T(8,128)S(1)}, s32[7,2]{1,0:T(8,128)S(1)}, u32[]{:S(2)}, u32[]{:S(2)}) collective-permute-start(s32[7,2]{1,0:T(8,128)S(1)} %pad_add_fusion.own_pos), channel_id=1, source_target_pairs={{1,0},{2,1},{3,2},{4,3},{5,4},{6,5},{7,6},{9,8},{10,9},{11,10},{12... | collective-permute-start | bytes 176 | tf_op jit(solution)/shard_map/ppermute | solution.py:32
  4.6 14.9 %collective-permute-start = (s32[7,2]{1,0:T(8,128)S(1)}, s32[7,2]{1,0:T(8,128)S(1)}, u32[]{:S(2)}, u32[]{:S(2)}) collective-permute-start(s32[7,2]{1,0:T(8,128)S(1)} %pad_add_fusion.own_pos), channel_id=1, source_target_pairs={{0,1},{1,2},{2,3},{3,4},{4,5},{5,6},{6,7},{8,9},{9,10},{10,11},{11... | collective-permute-start | bytes 176 | tf_op jit(solution)/shard_map/ppermute | solution.py:32
  19.5 0.6 copy-start.2
  19.5 0.6 copy-start.3
  221.4 10.4 %copy-start = (f32[6,2,256,256]{3,2,1,0:T(8,128)S(1)}, f32[6,2,256,256]{3,2,1,0:T(8,128)}, u32[]{:S(2)}) copy-start(f32[6,2,256,256]{3,2,1,0:T(8,128)} %get-tuple-element.12) | copy-start | bytes 9437188

commit v3 on v2

--- a/solution.py
+++ b/solution.py
@@ -3,6 +3,7 @@
 
 import jax
 import jax.numpy as jnp
+import numpy as np
 from jax import lax
 from jax.experimental import pallas as pl
 from jax.experimental.pallas import tpu as pltpu
@@ -33,24 +34,22 @@
 
 
 def make_tables(extent):
-    indices = jnp.arange(extent, dtype=jnp.int32)
-    product = indices[:, None] * indices[None, :] % extent
-    angles = product.astype(jnp.float32) * (2.0 * math.pi / extent)
-    cosine = jnp.cos(angles) / math.sqrt(extent)
-    sine = jnp.sin(angles) / math.sqrt(extent)
-
-    def split(x):
-        hi = lax.reduce_precision(x, 8, 7)
-        lo = x - hi
-        return hi.astype(jnp.bfloat16), lo.astype(jnp.bfloat16)
-
-    def square(c, s, sign):
-        return jnp.concatenate(
-            [jnp.concatenate([c, sign * s], 1), jnp.concatenate([-sign * s, c], 1)], 0
-        )
-
-    (ch, cl), (sh, sl) = split(cosine), split(sine)
-    return (square(ch, sh, 1), square(cl, sl, 1), square(ch, sh, -1), square(cl, sl, -1))
+    half = extent // 2
+    indices = np.arange(extent)
+    angles = (indices[:, None] * indices[None, :] % extent) * (2.0 * math.pi / extent)
+    cosine = (np.cos(angles) / math.sqrt(extent)).astype(np.float32)
+    sine = (np.sin(angles) / math.sqrt(extent)).astype(np.float32)
+    tables = []
+    for parity in range(2):
+        c, s = cosine[parity::2, :half], sine[parity::2, :half]
+        block = np.block([[c, s], [-s, c]])
+        for matrix in (block, block.T):
+            hi = matrix.astype(jnp.bfloat16)
+            lo = (matrix - hi.astype(np.float32)).astype(jnp.bfloat16)
+            tables += [jnp.asarray(hi), jnp.asarray(lo)]
+    order = np.concatenate([indices[0::2], indices[1::2]])
+    sort = (order[:, None] == indices[None, :]).astype(jnp.bfloat16)
+    return tables + [jnp.asarray(sort), jnp.asarray(np.ascontiguousarray(sort.T))]
 
 
 def aligned(row, limit):
@@ -166,17 +165,17 @@
 
 
 def pipeline_kernel(sections, tiles, live, to_left, to_right, own, probe, phase_kernel, measured,
-                    fwd_hi, fwd_lo, inv_hi, inv_lo, adjoint, contrib, from_left, from_right,
+                    ef_hi, ef_lo, ei_hi, ei_lo, of_hi, of_lo, oi_hi, oi_lo, sort, unsort, adjoint, contrib, from_left, from_right,
                     windows, left_rim, right_rim, got_left, got_right,
-                    arrived, leaving, backed, left_f, left_i, right_f, right_i,
-                    tall_b, wide_b, spectrum, send_f, recv_f, send_b, recv_b,
+                    arrived, leaving, backed, lefts, rights, turn,
+                    talls, wides, freq, spectrum, send_f, recv_f, send_b, recv_b,
                     send_rim, recv_rim, send_got, recv_got):
     g = lax.axis_index("cuts")
     t = lax.axis_index("tile")
     last = sections - 1
     end = tiles - 1
     slots, _, extent, _ = own.shape
-    two = 2 * extent
+    h = extent // 2
 
     barrier = pltpu.get_barrier_semaphore()
 
@@ -195,15 +194,6 @@
     @pl.when(t < end)
     def _():
         pl.semaphore_signal(barrier, inc=1, device_id={"tile": t + 1}, device_id_type=MESH)
-
-    for table, hi, lo in ((left_f, fwd_hi, fwd_lo), (left_i, inv_hi, inv_lo)):
-        table[:, :two] = hi[...]
-        table[:, two : 2 * two] = hi[...]
-        table[:, 2 * two :] = lo[...]
-    for table, hi, lo in ((right_f, inv_hi, inv_lo), (right_i, fwd_hi, fwd_lo)):
-        table[:two] = hi[...]
-        table[two : 2 * two] = hi[...]
-        table[2 * two :] = lo[...]
 
     peers = (g + last - 1) // last + 1 - g // last + (t + end - 1) // end + 1 - t // end
     pl.semaphore_wait(barrier, peers)
@@ -247,33 +237,88 @@
         right_rim[...] = jnp.zeros(right_rim.shape, right_rim.dtype)
         got_right[...] = jnp.zeros(got_right.shape, got_right.dtype)
 
-    def put(ref, rows, p, value):
+    forms = ((ef_hi, ef_lo, ei_hi, ei_lo), (of_hi, of_lo, oi_hi, oi_lo))
+    for parity in range(2):
+        fh, fl, ih, il = forms[parity]
+        for inverse, (lh, ll, rh, rl) in enumerate(((fh, fl, ih, il), (ih, il, fh, fl))):
+            at = 2 * inverse + parity
+            lefts[at, :, :extent] = lh[...]
+            lefts[at, :, extent : 2 * extent] = lh[...]
+            lefts[at, :, 2 * extent :] = ll[...]
+            rights[at, :extent] = rh[...]
+            rights[at, extent : 2 * extent] = rh[...]
+            rights[at, 2 * extent :] = rl[...]
+
+    def exact(x, y):
+        return jnp.dot(x, y, preferred_element_type=jnp.float32)
+
+    for p in range(2):
+        rest = phase_kernel[p]
+        total = jnp.zeros((extent, extent), jnp.float32)
+        for _ in range(3):
+            part = rest.astype(jnp.bfloat16)
+            rest = rest - part.astype(jnp.float32)
+            rows = exact(sort[...], part).astype(jnp.bfloat16)
+            total += exact(rows, unsort[...])
+        turn[p] = total
+
+    def split(value):
         hi = value.astype(jnp.bfloat16)
         lo = (value - hi.astype(jnp.float32)).astype(jnp.bfloat16)
-        n = value.shape[0 if rows else 1]
-        for at, part in ((0, hi), (1, lo), (2, hi)):
-            place = pl.ds(at * two + p * n, n)
-            if rows:
-                ref[place, :] = part
-            else:
-                ref[:, place] = part
-
-    def transform(left, right):
-        half = jnp.dot(left[...], tall_b[...], preferred_element_type=jnp.float32)
-        put(wide_b, False, 0, half[:extent])
-        put(wide_b, False, 1, half[extent:])
-        spectrum[...] = jnp.dot(wide_b[...], right[...], preferred_element_type=jnp.float32)
-
-    def times_kernel(sign):
-        kr, ki = phase_kernel[0], sign * phase_kernel[1]
-        xr, xi = spectrum[:, :extent], spectrum[:, extent:]
-        put(tall_b, True, 0, kr * xr - ki * xi)
-        put(tall_b, True, 1, kr * xi + ki * xr)
-
-    def propagate(sign):
-        transform(left_f, right_f)
-        times_kernel(sign)
-        transform(left_i, right_i)
+        return (hi, lo, hi)
+
+    def put_tall(parity, p, value):
+        for at, part in enumerate(split(value)):
+            talls[parity, pl.ds(at * extent + p * h, h), :] = part
+
+    def put_wide(parity, rows, p, value):
+        n = value.shape[0]
+        for at, part in enumerate(split(value)):
+            wides[parity, pl.ds(rows, n), pl.ds(at * extent + p * h, h)] = part
+
+    def left(at):
+        return exact(lefts[at], talls[at % 2])
+
+    def right(at):
+        return exact(wides[at % 2], rights[at])
+
+    def to_freq(pair):
+        for p in range(2):
+            put_tall(0, p, pair[p][:h] + pair[p][h:])
+            put_tall(1, p, pair[p][:h] - pair[p][h:])
+        for block in range(2):
+            half = left(block)
+            for p in range(2):
+                value = half[p * h : (p + 1) * h]
+                put_wide(0, block * h, p, value[:, :h] + value[:, h:])
+                put_wide(1, block * h, p, value[:, :h] - value[:, h:])
+        for parity in range(2):
+            freq[parity] = right(parity)
+
+    def from_freq():
+        u, v = right(2), right(3)
+        for p in range(2):
+            up, vp = u[:, p * h : (p + 1) * h], v[:, p * h : (p + 1) * h]
+            plus, minus = up + vp, up - vp
+            for parity in range(2):
+                rows = slice(parity * h, (parity + 1) * h)
+                both = jnp.concatenate([plus[rows], minus[rows]], axis=1)
+                put_tall(parity, p, both)
+        u, v = left(2), left(3)
+        for p in range(2):
+            up, vp = u[p * h : (p + 1) * h], v[p * h : (p + 1) * h]
+            spectrum[p, :h] = up + vp
+            spectrum[p, h:] = up - vp
+
+    def propagate(pair, sign):
+        to_freq(pair)
+        for parity in range(2):
+            cols = slice(parity * h, (parity + 1) * h)
+            kr, ki = turn[0, :, cols], sign * turn[1, :, cols]
+            xr, xi = freq[parity, :, :h], freq[parity, :, h:]
+            put_wide(parity, 0, 0, kr * xr - ki * xi)
+            put_wide(parity, 0, 1, kr * xi + ki * xr)
+        from_freq()
 
     def send_forward(s):
         return pltpu.make_async_remote_copy(
@@ -309,38 +354,35 @@
             windows[s, p, :, extent - RIM :] = own[s, p, :, extent - RIM :] + right_rim[s, p]
         wr, wi = windows[s, 0], windows[s, 1]
         xr, xi = arrived[s, 0], arrived[s, 1]
-        put(tall_b, True, 0, wr * xr - wi * xi)
-        put(tall_b, True, 1, wr * xi + wi * xr)
-        propagate(1.0)
+        propagate((wr * xr - wi * xi, wr * xi + wi * xr), 1.0)
 
         @pl.when(g < last)
         def _():
-            leaving[s, 0] = spectrum[:, :extent]
-            leaving[s, 1] = spectrum[:, extent:]
+            leaving[s, 0] = spectrum[0]
+            leaving[s, 1] = spectrum[1]
             send_forward(s).start()
 
     def backward(s):
         @pl.when(g == last)
         def _():
-            put(tall_b, True, 0, spectrum[:, :extent])
-            put(tall_b, True, 1, spectrum[:, extent:])
-            transform(left_f, right_f)
-            fr, fi = spectrum[:, :extent], spectrum[:, extent:]
-            residual = fr * fr + fi * fi - measured[s].astype(jnp.float32)
-            put(tall_b, True, 0, fr * residual)
-            put(tall_b, True, 1, fi * residual)
-            transform(left_i, right_i)
-            put(tall_b, True, 0, spectrum[:, :extent])
-            put(tall_b, True, 1, spectrum[:, extent:])
+            seen = exact(sort[...], measured[s]).astype(jnp.bfloat16)
+            seen = exact(seen, unsort[...])
+            to_freq((spectrum[0], spectrum[1]))
+            for parity in range(2):
+                fr, fi = freq[parity, :, :h], freq[parity, :, h:]
+                residual = fr * fr + fi * fi - seen[:, parity * h : (parity + 1) * h]
+                put_wide(parity, 0, 0, fr * residual)
+                put_wide(parity, 0, 1, fi * residual)
+            from_freq()
 
         @pl.when(g < last)
         def _():
             send_backward(s).wait_recv()
-            put(tall_b, True, 0, backed[s, 0])
-            put(tall_b, True, 1, backed[s, 1])
-
-        propagate(-1.0)
-        tr, ti = spectrum[:, :extent], spectrum[:, extent:]
+            spectrum[0] = backed[s, 0]
+            spectrum[1] = backed[s, 1]
+
+        propagate((spectrum[0], spectrum[1]), -1.0)
+        tr, ti = spectrum[0], spectrum[1]
         wr, wi = windows[s, 0], windows[s, 1]
         br, bi = wr * tr + wi * ti, wr * ti - wi * tr
 
@@ -450,24 +492,23 @@
     phase_kernel = jnp.stack([jnp.cos(kernel_phase), jnp.sin(kernel_phase)], 0)
     live = (jnp.arange(slots, dtype=jnp.int32) < counts[0]).astype(f32)
     waves = pltpu.VMEM((slots, 2, extent, extent), f32)
-    two = 2 * extent
     bf16 = jnp.bfloat16
     rims = pltpu.VMEM((slots, 2, extent, RIM), f32)
     adjoint, contrib, from_left, from_right = pl.pallas_call(
         functools.partial(pipeline_kernel, sections, tiles_total),
         out_shape=(wave, wave, rim, rim),
-        in_specs=[smem()] + [vmem()] * 10,
+        in_specs=[smem()] + [vmem()] * 16,
         out_specs=(vmem(),) * 4,
         scratch_shapes=[
             waves, rims, rims, rims, rims,
             waves, waves, waves,
-            pltpu.VMEM((two, 3 * two), bf16),
-            pltpu.VMEM((two, 3 * two), bf16),
-            pltpu.VMEM((3 * two, two), bf16),
-            pltpu.VMEM((3 * two, two), bf16),
-            pltpu.VMEM((3 * two, extent), bf16),
-            pltpu.VMEM((extent, 3 * two), bf16),
-            pltpu.VMEM((extent, two), f32),
+            pltpu.VMEM((4, extent, 3 * extent), bf16),
+            pltpu.VMEM((4, 3 * extent, extent), bf16),
+            pltpu.VMEM((2, extent, extent), f32),
+            pltpu.VMEM((2, 3 * extent, extent), bf16),
+            pltpu.VMEM((2, extent, 3 * extent), bf16),
+            pltpu.VMEM((2, extent, extent), f32),
+            pltpu.VMEM((2, extent, extent), f32),
             pltpu.SemaphoreType.DMA((slots,)),
             pltpu.SemaphoreType.DMA((slots,)),
             pltpu.SemaphoreType.DMA((slots,)),

time: 234 us -> 202 us (0.86)
  Pallas kernels: 212 us -> 186 us
  other arithmetic: 9.11 us -> 2.73 us
    pallas_call x1, Pallas kernels: 193 us -> 167 us  [on_device(): pl.pallas_call(functools.partial(pipeline_kernel, sections, tiles_total),...]
  transfers between devices with their start and end apart: 2 -> 2, of which waited for: 0 -> 0; matrix products, arithmetic and copies ran while one was open for 4% -> 2% of each run, Pallas kernels for 0% -> 0%
where the time goes in v3:
time: 202 us
  Pallas kernels  186 us (92%)
  starting transfers between devices  6.46 us (3%)
  local copies, waits for them, and re-layouts  4.86 us (2%)
  other arithmetic  2.73 us (1%)
    pallas_call x1, Pallas kernels, on_device(): pl.pallas_call(functools.partial(pipeline_kernel, sections, tiles_total),...  167 us
    pallas_call x1, Pallas kernels, on_device(): pl.pallas_call(gather_kernel, out_shape=sds((2, rows, cols), f32), in_spe...  10.3 us
    pallas_call x1, Pallas kernels, on_device(): pl.pallas_call(extract_kernel, out_shape=(wave, rim, rim), in_specs=[smem...  8.66 us
    ppermute x2, starting transfers between devices, shift(): return lax.ppermute(value, axis, pairs)  6.46 us
  transfers between devices with their start and end apart: 2, of which 0 were waited for; matrix products, arithmetic and copies ran while one was open for 2% of the time, Pallas kernels for 0%

profile of v3, /device:TPU:3, one launch (start us, length us, event | category | flops | bytes accessed | tf_op | source)
XLA Modules:
  0.0 201.6 jit_solution(18379106596921026202)
XLA Ops:
  0.6 0.8 copy.25
  1.4 0.7 pad_add_fusion.own_pos
  2.1 0.0 copy-start.1
  2.1 2.6 %collective-permute-start.1 = (s32[7,2]{1,0:T(8,128)S(1)}, s32[7,2]{1,0:T(8,128)S(1)}, u32[]{:S(2)}, u32[]{:S(2)}) collective-permute-start(s32[7,2]{1,0:T(8,128)S(1)} %pad_add_fusion.own_pos), channel_id=1, source_target_pairs={{1,0},{2,1},{3,2},{4,3},{5,4},{6,5},{7,6},{9,8},{10,9},{11,10},{12... | collective-permute-start | bytes 176 | tf_op jit(solution)/shard_map/ppermute | solution.py:33
  4.6 3.9 %collective-permute-start = (s32[7,2]{1,0:T(8,128)S(1)}, s32[7,2]{1,0:T(8,128)S(1)}, u32[]{:S(2)}, u32[]{:S(2)}) collective-permute-start(s32[7,2]{1,0:T(8,128)S(1)} %pad_add_fusion.own_pos), channel_id=1, source_target_pairs={{0,1},{1,2},{2,3},{3,4},{4,5},{5,6},{6,7},{8,9},{9,10},{10,11},{11... | collective-permute-start | bytes 176 | tf_op jit(solution)/shard_map/ppermute | solution.py:33
  9.2 0.6 compare_convert_fusion.live
  9.8 1.9 cosine_bitcast_fusion
  11.6 0.8 pad_maximum_fusion.phase_kernel
  12.5 0.7 pad_add_fusion.1.here
  13.1 0.0 collective-permute-done.1.right_pos
  13.1 0.0 copy-start.2
  13.1 0.0 collective-permute-done.left_pos
  13.1 0.0 copy-start.3
  13.1 0.0 copy-done.1
  13.1 0.6 copy-done.2
  13.7 0.0 copy-done.3
  13.7 8.7 %shard_map.176 = (f32[6,2,256,256]{3,2,1,0:T(8,128)}, f32[6,2,256,128]{3,2,1,0:T(8,128)}, f32[6,2,256,128]{3,2,1,0:T(8,128)}) custom-call(s32[2]{0:T(128)} %pad_add_fusion.1.here, s32[7,2]{1,0:T(8,128)} %copy-done.3, s32[7,2]{1,0:T(8,128)} %copy-done.2, s32[7,2]{1,0:T(8,128)} %copy-done.1, f32[2,4096,256]{2,1,0:T(8,128)} %bitcast.12), custom_call_target="tpu_custom_call" | custom-call | tf_op jit(solution)/shard_map/pallas_call | solution.py:477
  22.4 167.2 %shard_map.177 = (f32[6,2,256,256]{3,2,1,0:T(8,128)}, f32[6,2,256,256]{3,2,1,0:T(8,128)}, f32[6,2,256,128]{3,2,1,0:T(8,128)}, f32[6,2,256,128]{3,2,1,0:T(8,128)}) custom-call(f32[6]{0:T(128)} %compare_convert_fusion.live, f32[6,2,256,128]{3,2,1,0:T(8,128)} %get-tuple-element.9.to_left, f32[6,2,256,128]{3,2,1,0:T(8,128)} %get-tuple-element.10.to_right, ...), custom_call_target="tpu_custom_call" | custom-call | tf_op jit(solution)/shard_map/pallas_call | solution.py:497
  189.6 0.0 copy-start
  189.6 10.3 %shard_map.178 = f32[2,4096,256]{2,1,0:T(8,128)} custom-call(s32[7,2]{1,0:T(8,128)} %copy-done.3, s32[7,2]{1,0:T(8,128)} %copy-done.2, s32[7,2]{1,0:T(8,128)} %copy-done.1, f32[6,2,256,256]{3,2,1,0:T(8,128)} %get-tuple-element.13.contrib, f32[6,2,256,128]{3,2,1,0:T(8,128)} %get-tuple-element.14.from_left, f32[6,2,256,128]{3,2,1,0:T(8,128)} %get-tuple-element.15.from_right), custom_call_target="tpu_custom_call" | custom-call | tf_op jit(solution)/shard_map/pallas_call | solution.py:524
  200.0 0.0 copy-done
  200.0 1.7 copy.28
Async XLA Ops:
  2.1 11.1 %copy-start.1 = (s32[7,2]{1,0:T(8,128)}, s32[7,2]{1,0:T(8,128)S(1)}, u32[]{:S(2)}) copy-start(s32[7,2]{1,0:T(8,128)S(1)} %pad_add_fusion.own_pos) | copy-start | bytes 172
  2.1 11.1 %collective-permute-start.1 = (s32[7,2]{1,0:T(8,128)S(1)}, s32[7,2]{1,0:T(8,128)S(1)}, u32[]{:S(2)}, u32[]{:S(2)}) collective-permute-start(s32[7,2]{1,0:T(8,128)S(1)} %pad_add_fusion.own_pos), channel_id=1, source_target_pairs={{1,0},{2,1},{3,2},{4,3},{5,4},{6,5},{7,6},{9,8},{10,9},{11,10},{12... | collective-permute-start | bytes 176 | tf_op jit(solution)/shard_map/ppermute | solution.py:33
  4.6 8.5 %collective-permute-start = (s32[7,2]{1,0:T(8,128)S(1)}, s32[7,2]{1,0:T(8,128)S(1)}, u32[]{:S(2)}, u32[]{:S(2)}) collective-permute-start(s32[7,2]{1,0:T(8,128)S(1)} %pad_add_fusion.own_pos), channel_id=1, source_target_pairs={{0,1},{1,2},{2,3},{3,4},{4,5},{5,6},{6,7},{8,9},{9,10},{10,11},{11... | collective-permute-start | bytes 176 | tf_op jit(solution)/shard_map/ppermute | solution.py:33
  13.1 0.6 copy-start.2
  13.1 0.6 copy-start.3
  189.6 10.4 %copy-start = (f32[6,2,256,256]{3,2,1,0:T(8,128)S(1)}, f32[6,2,256,256]{3,2,1,0:T(8,128)}, u32[]{:S(2)}) copy-start(f32[6,2,256,256]{3,2,1,0:T(8,128)} %get-tuple-element.12) | copy-start | bytes 9437188
